TPU v7x, 32 devices: a whole 2x2x4 slice. The times are simulated.
32 devices in a mesh: blk: 16 (over z, y, core), along: 2 (over x).
Axes of the slice: x: 2, y: 2, z: 4, core: 2. Of those that a mesh axis runs over, the one named last changes fastest.
Arguments:
- values: float32 [3, 16, 48, 256], P(None, 'blk', 'along'), may hold values from -6 to 6
- offsets: float32 [3, 16, 48, 256], P(None, 'blk', 'along'), may hold values from 0 to 1
- stiffness: float32 [16, 48, 256], P('blk', 'along'), may hold values from 0.5 to 2
- leaf_basis: float32 [16, 48, 64, 256], P('blk', 'along'), may hold values from -0.375 to 0.375
- transfer: float32 [16, 48, 64, 64], P('blk', 'along'), may hold values from -0.15625 to 0.15625
- slab_transfer_matrices: float32 [16, 2, 64, 64], P('blk', 'along'), may hold values from -0.5 to 0.5
- leaf_coupling_matrices: float32 [16, 30, 64, 64], P('blk'), may hold values from -0.375 to 0.375
- leaf_admissible_mask: int32 [16, 30], P('blk'), may hold values 0 or 1
- top_coupling: float32 [16, 16, 64, 64], P('blk'), may hold values from -0.75 to 0.75
- top_admissible: int32 [16, 16], P('blk'), may hold values 0 or 1
Outputs:
- product: float32 [3, 16, 48, 256], P(None, 'blk', 'along')
All inputs are finite; a program needn't handle non-finite values. No bound on the sum of `leaf_admissible_mask` or of `top_admissible` on one device may be relied on, other than what follows from the above.
Results may differ from a plain program's by a relative error of at most 0.0001.
Values sent between devices are 32-bit elements; how exact they have to be, the bound alone decides.
A program may use at most 64 MiB of HBM per device.

v0:
```python
import functools

import jax
import jax.numpy as jnp
from jax import lax
from jax.experimental import pallas as pl
from jax.experimental.pallas import tpu as pltpu
from jax.sharding import PartitionSpec as P

REACH = 6


SHARPNESS = 2.0
KERNEL_SCALE = 0.125
HIGHEST_ACCURACY = lax.Precision.HIGHEST


def split_in_two(x):
    high = x.astype(jnp.bfloat16).astype(jnp.float32)
    return high, x - high


def near_steps(cells_ref, out_ref, feature_ref, weight_ref):
    leaves, _, size = out_ref.shape
    row = lax.broadcasted_iota(jnp.int32, (8, size), 0)
    log2e = 1.4426950408889634

    def prepare(a):
        def step(m, carry):
            cell = cells_ref[a, m]
            high, low = split_in_two(jnp.where(row < 3, cell, 0.0))
            stacked = jnp.concatenate([high, low, high, low], 0)
            feature_ref[a, m] = stacked.T.astype(jnp.bfloat16)
            around = cell[0:1] + (a - 1.0)
            radial = cell[2:3]
            part = around * around + radial * radial
            for b in range(3):
                along = cell[1:2] + (b - 1.0)
                factor = jnp.exp2((-SHARPNESS * log2e) * (part + along * along))
                high, low = split_in_two(cell * factor)
                weight_ref[a, m, b] = jnp.concatenate([high, low], 0).astype(jnp.bfloat16)
            return carry

        lax.fori_loop(0, leaves + 2, step, 0)

    def leaf(sources, first, m, carry):
        cell = cells_ref[1, m + 1]
        high, low = split_in_two(jnp.where(row < 3, cell * (2 * SHARPNESS * log2e), 0.0))
        target = jnp.concatenate([high, high, low, low], 0).astype(jnp.bfloat16)
        x0, x1, x2 = cell[0:1], cell[1:2], cell[2:3]
        base = (
            KERNEL_SCALE
            * cell[6:7]
            * jnp.exp2((-SHARPNESS * log2e) * (x0 * x0 + x1 * x1 + x2 * x2))
        )
        total = jnp.zeros((8, size), jnp.float32) if first else out_ref[m]
        for a in sources:
            for b in range(3):
                power = jnp.dot(
                    feature_ref[a, m + b], target, preferred_element_type=jnp.float32
                )
                tile = jnp.exp2(power)
                tile_high = tile.astype(jnp.bfloat16)
                tile_low = (tile - tile_high.astype(jnp.float32)).astype(jnp.bfloat16)
                weight = weight_ref[a, m + b, b]
                got = jnp.dot(weight, tile_high, preferred_element_type=jnp.float32) + jnp.dot(
                    weight, tile_low, preferred_element_type=jnp.float32
                )
                factor = base * jnp.exp2(
                    (2 * SHARPNESS * log2e) * ((a - 1.0) * x0 + (b - 1.0) * x1)
                )
                total = total + factor * (got[:8] + got[8:])
        out_ref[m] = total
        return carry

    def run(sources, first):
        for a in sources:
            prepare(a)
        lax.fori_loop(0, leaves, functools.partial(leaf, sources, first), 0)

    return run


def far_offsets():
    ahead = list(range(2, REACH + 1))
    return ahead + [-step for step in ahead]


def exchange_kernel(
    cells_ref,
    coefs_ref,
    ends_ref,
    share_ref,
    near_ref,
    windows_ref,
    rims_ref,
    shares_ref,
    padded_ref,
    feature_ref,
    weight_ref,
    send_sem,
    recv_sem,
    share_send_sem,
    share_recv_sem,
):
    sectors, slabs = lax.axis_size("blk"), lax.axis_size("along")
    sector, slab = lax.axis_index("blk"), lax.axis_index("along")
    leaves = cells_ref.shape[0]
    copies = []

    def send(source, target, around, along):
        k = len(copies)
        copy = pltpu.make_async_remote_copy(
            src_ref=source,
            dst_ref=target,
            send_sem=send_sem.at[k],
            recv_sem=recv_sem.at[k],
            device_id={
                "blk": lax.rem(sector + around + sectors, sectors),
                "along": lax.rem(slab + along + slabs, slabs),
            },
            device_id_type=pl.DeviceIdType.MESH,
        )
        copy.start()
        copies.append(copy)

    distant = sectors - 2 * REACH - 1

    def share_copy(k, row, column):
        return pltpu.make_async_remote_copy(
            src_ref=share_ref,
            dst_ref=shares_ref.at[row, column],
            send_sem=share_send_sem.at[k],
            recv_sem=share_recv_sem.at[k // slabs * slabs + column],
            device_id={
                "blk": lax.rem(sector + REACH + 1 + k // slabs, sectors),
                "along": lax.rem(k, slabs),
            },
            device_id_type=pl.DeviceIdType.MESH,
        )

    def share_start(k, carry):
        share_copy(k, sector, slab).start()
        return carry

    def share_wait(k, carry):
        came = lax.rem(sector + sectors - REACH - 1 - k // slabs, sectors)
        share_copy(k, sector, slab).wait_send()
        share_copy(k, came, lax.rem(k, slabs)).wait_recv()
        return carry

    for around in (0, -1, 1):
        send(cells_ref.at[leaves - 1], padded_ref.at[1 - around, 0], around, 1)
        send(cells_ref.at[0], padded_ref.at[1 - around, leaves + 1], around, -1)
    for around in (-1, 1):
        send(cells_ref, padded_ref.at[1 - around, pl.ds(1, leaves)], around, 0)
    lax.fori_loop(0, distant * slabs, share_start, 0)
    for q, around in enumerate(far_offsets()):
        send(coefs_ref, windows_ref.at[q], -around, 0)
        send(ends_ref.at[1], rims_ref.at[q, 0], -around, 1)
        send(ends_ref.at[0], rims_ref.at[q, 1], -around, -1)
    padded_ref[1, pl.ds(1, leaves)] = cells_ref[...]
    run = near_steps(padded_ref, near_ref, feature_ref, weight_ref)

    def close(a):
        @pl.when(slab == 0)
        def _():
            padded_ref[a, 0] = jnp.zeros_like(padded_ref[a, 0])

        @pl.when(slab == slabs - 1)
        def _():
            padded_ref[a, leaves + 1] = jnp.zeros_like(padded_ref[a, 0])

    for copy in copies[:2]:
        copy.wait()
    close(1)
    run((1,), True)
    for copy in copies[2:8]:
        copy.wait()
    close(0)
    close(2)
    run((0, 2), False)
    for copy in copies[8:]:
        copy.wait()
    lax.fori_loop(0, distant * slabs, share_wait, 0)

    @pl.when(slab == 0)
    def _():
        rims_ref[:, 0] = jnp.zeros_like(rims_ref[:, 0])

    @pl.when(slab == slabs - 1)
    def _():
        rims_ref[:, 1] = jnp.zeros_like(rims_ref[:, 1])


def exchange(cells, coefs, ends, share):
    sectors, slabs = lax.axis_size("blk"), lax.axis_size("along")
    leaves, _, size = cells.shape
    far = 2 * (REACH - 1)
    links = 8 + 3 * far
    pairs = (sectors - 2 * REACH - 1) * slabs
    vmem = pl.BlockSpec(memory_space=pltpu.VMEM)
    return pl.pallas_call(
        exchange_kernel,
        out_shape=(
            jax.ShapeDtypeStruct((leaves, 8, size), jnp.float32),
            jax.ShapeDtypeStruct((far, *coefs.shape), jnp.float32),
            jax.ShapeDtypeStruct((far, *ends.shape), jnp.float32),
            jax.ShapeDtypeStruct((sectors, slabs, *share.shape), jnp.float32),
        ),
        in_specs=[vmem] * 4,
        out_specs=(vmem,) * 4,
        scratch_shapes=[
            pltpu.VMEM((3, leaves + 2, 8, size), jnp.float32),
            pltpu.VMEM((3, leaves + 2, size, 32), jnp.bfloat16),
            pltpu.VMEM((3, leaves + 2, 3, 16, size), jnp.bfloat16),
            pltpu.SemaphoreType.DMA((links,)),
            pltpu.SemaphoreType.DMA((links,)),
            pltpu.SemaphoreType.DMA((pairs,)),
            pltpu.SemaphoreType.DMA((pairs,)),
        ],
        compiler_params=pltpu.CompilerParams(
            has_side_effects=True, vmem_limit_bytes=40 * 1024 * 1024
        ),
    )(cells, coefs, ends, share)


def body(
    values,
    offsets,
    stiffness,
    leaf_basis,
    transfer,
    slab_transfer_matrices,
    leaf_coupling_matrices,
    leaf_admissible_mask,
    top_coupling,
    top_admissible,
):
    cells = jnp.concatenate(
        [
            offsets - 0.5,
            stiffness[None] * values,
            stiffness[None],
            jnp.zeros_like(stiffness)[None],
        ],
        0,
    ).transpose(1, 2, 0, 3)
    coefs = jnp.einsum("slki,rsli->rslk", leaf_basis, values, precision=HIGHEST_ACCURACY)
    slab_coefficient_rows = jnp.einsum(
        "slqk,rslq->rsk", transfer, coefs, precision=HIGHEST_ACCURACY
    )
    shared_portion = jnp.einsum(
        "oxz,eox->eoz",
        slab_transfer_matrices[:, 0],
        slab_coefficient_rows,
        precision=HIGHEST_ACCURACY,
    )
    by_leaf = coefs[:, 0].transpose(1, 0, 2)
    leaves, count, rank = by_leaf.shape
    width = -(-count * rank // 128) * 128
    lanes = -(-rank // 128) * 128
    flat = by_leaf.reshape(leaves, count * rank)
    ends = jnp.stack([by_leaf[0], by_leaf[-1]])
    near, windows, rims, shares = exchange(
        cells[0],
        jnp.pad(flat, ((0, 0), (0, width - count * rank))),
        jnp.pad(ends, ((0, 0), (0, 8 - count), (0, lanes - rank))),
        jnp.pad(shared_portion[:, 0], ((0, 8 - count), (0, lanes - rank))),
    )
    near = near[:, 3:6].transpose(1, 0, 2)[:, None]
    far = windows.shape[0]
    windows = windows[:, :, : count * rank].reshape(far, leaves, count, rank)
    rims = rims[:, :, :count, :rank]
    windows = jnp.concatenate([rims[:, :1], windows, rims[:, 1:]], 1)
    partners = jnp.stack([windows[:, b : b + leaves] for b in range(3)], 1)
    coupling = (
        leaf_coupling_matrices[0] * leaf_admissible_mask[0].astype(jnp.float32)[:, None, None]
    ).reshape(far, 3, rank, rank)
    far_leaf = jnp.einsum(
        "qbkz,qblrz->rlk", coupling, partners, precision=HIGHEST_ACCURACY
    )[:, None]
    sectors = lax.axis_size("blk")
    sector = lax.axis_index("blk")
    others = jnp.arange(sectors, dtype=jnp.int32)
    apart = (others - sector) % sectors
    distant = jnp.logical_and(apart > REACH, apart < sectors - REACH)
    allowed = jnp.where(distant, top_admissible[0].astype(jnp.float32), 0.0)
    shares = jnp.where(distant[:, None, None, None], shares, 0.0)
    every_sector = shares.sum(1)[:, :count, :rank].transpose(1, 0, 2)
    sector_local_coefs = jnp.einsum(
        "stkq,rtq->rsk",
        top_coupling * allowed[None, :, None, None],
        every_sector,
        precision=HIGHEST_ACCURACY,
    )
    slab_local_coefs = jnp.einsum(
        "baz,lbz->lba", slab_transfer_matrices[:, 0], sector_local_coefs, precision=HIGHEST_ACCURACY
    )
    leaf_down = jnp.einsum("slqk,rsk->rslq", transfer, slab_local_coefs, precision=HIGHEST_ACCURACY)
    leaf_local = far_leaf + leaf_down
    return near + jnp.einsum("slki,rslk->rsli", leaf_basis, leaf_local, precision=HIGHEST_ACCURACY)


def solution(mesh):
    return jax.shard_map(
        body,
        mesh=mesh,
        in_specs=(
            P(None, "blk", "along", None),
            P(None, "blk", "along", None),
            P("blk", "along", None),
            P("blk", "along", None, None),
            P("blk", "along", None, None),
            P("blk", "along", None, None),
            P("blk", None, None, None),
            P("blk", None),
            P("blk", None, None, None),
            P("blk", None),
        ),
        out_specs=P(None, "blk", "along", None),
        check_vma=False,
    )
```

profile of v0, /device:TPU:0, one launch (start us, length us, event | category | flops | bytes accessed | tf_op | source)
XLA Modules:
  0.0 61.6 jit_solution(10763149204247725594)
XLA Ops:
  0.0 0.0 copy-start
  0.0 0.0 copy-start.5
  0.0 0.0 copy-start.1
  0.0 0.0 copy-start.6
  0.0 0.0 copy-start.4
  0.0 0.0 copy-start.7
  0.0 0.8 %convert_reduce_fusion = f32[30]{0:T(128)S(1)} fusion(s32[1,30]{1,0:T(1,128)} %param.17), kind=kLoop, calls=%fused_computation.49 | loop fusion | flops 30 | bytes 240 | tf_op jit(solution)/shard_map/convert_element_type | solution.py:278
  0.9 0.7 %bitcast_select_fusion = f32[16]{0:T(128)S(1)} fusion(s32[1,16]{1,0:T(1,128)} %param.19, s32[]{:T(128)S(6)} %axis_index.15), kind=kLoop, calls=%fused_computation.48 | loop fusion | flops 272 | bytes 132 | tf_op jit(solution)/shard_map/jit(_where)/select_n | solution.py:288
  1.5 0.1 pad.27.clone
  1.6 0.1 convert_element_type.27
  1.7 0.1 copy.28
  1.8 0.8 %broadcast_in_dim.27 = f32[1,1,24,256]{3,0,2,1:T(1,128)S(1)} reshape(f32[1,24,256]{2,1,0:T(8,128)} %param.12) | data formatting | bytes 49152 | tf_op jit(solution)/shard_map/broadcast_in_dim | solution.py:243
  2.6 0.0 copy-done
  2.6 2.3 %fusion.2 = f32[24,3,64]{2,1,0:T(4,128)S(1)} fusion(f32[1,24,64,256]{3,2,1,0:T(8,128)S(1)} %copy-done, f32[3,24,256]{2,1,0:T(8,128)} %bitcast.86), kind=kOutput, calls=%fused_computation.2 | convolution fusion | flops 14155776 | bytes 1665024 | tf_op jit(solution)/shard_map/slki,rsli->rslk/dot_general | solution.py:249
  4.8 0.0 copy-done.1
  4.8 0.0 copy-start.3
  4.8 0.5 convolution_bitcast_fusion.3
  5.4 0.0 copy-done.5
  5.4 0.1 fusion.30
  5.5 0.1 reshape.109
  5.6 0.0 copy-done.6
  5.7 0.0 copy-done.4
  5.7 0.0 copy-done.7
  5.7 0.1 copy_multiply_fusion.2
  5.8 0.1 maximum_bitcast_fusion.cells_ref
  5.9 48.5 %shard_map.100 = (f32[24,8,256]{2,1,0:T(8,128)S(1)}, f32[10,24,256]{2,1,0:T(8,128)S(1)}, f32[10,2,8,128]{3,2,1,0:T(8,128)S(1)}, f32[16,2,8,128]{3,2,1,0:T(8,128)S(1)}) custom-call(f32[24,8,256]{2,1,0:T(8,128)S(1)} %maximum_bitcast_fusion.cells_ref, f32[24,256]{1,0:T(8,128)S(1)} %pad.12.coefs_ref, f32[2,8,128]{2,1,0:T(8,128)S(1)} %select_maximum_fusion.ends_ref, ...), custom_call_target="tpu_custom_call" | custom-call | tf_op jit(solution)/shard_map/pallas_call | solution.py:203
  54.4 0.1 select_reduce_fusion
  54.5 0.0 copy-done.3
  54.5 0.6 convolution_bitcast_fusion.1
  55.1 0.2 convolution_bitcast_fusion.2
  55.3 1.9 %fusion.17 = f32[3,24,64]{2,0,1:T(4,128)S(1)} fusion(f32[3,64,1]{1,0,2:T(4,128)S(1)} %convolution_bitcast_fusion.2, f32[1,24,64,64]{3,2,1,0:T(8,128)S(1)} %copy-done.1), kind=kOutput, calls=%fused_computation.18 | convolution fusion | flops 3538944 | bytes 412416 | tf_op jit(solution)/shard_map/slqk,rsk->rslq/dot_general | solution.py:300
  57.2 0.2 stack_reshape.3
  57.5 0.2 reshape.113
  57.7 0.0 copy-start.2
  57.7 0.1 fusion.24
  57.8 1.1 %copy-done.2 = f32[1,30,64,64]{3,2,1,0:T(8,128)S(1)} copy-done((f32[1,30,64,64]{3,2,1,0:T(8,128)S(1)}, f32[1,30,64,64]{3,2,1,0:T(8,128)}, u32[]{:S(2)}) %copy-start.2) | copy-done | bytes 491544
  58.9 1.2 %fusion.10 = f32[3,24,64]{2,1,0:T(8,128)S(1)} fusion(f32[10,1,24,3,64]{4,2,0,1,3:T(8,128)S(1)} %get-tuple-element.14, f32[10,1,24,3,64]{4,2,0,1,3:T(8,128)S(1)} %copy.27, f32[10,1,24,3,64]{4,2,0,1,3:T(8,128)S(1)} %get-tuple-element.13, f32[10,3,64,64]{3,2,1,0:T(8,128)S(1)} %bitcast.85, f32[10,3]{0,1:T(4,128)S(1)} %copy.28, f32[3,24,64]{2,0,1:T(4,128)S(1)} %fusion.17), kind=kOutput, calls=%fused_computation.7 | convolution fusion | flops 106572288 | bytes 1081464 | tf_op jit(solution)/shard_map/qbkz,qblrz->rlk/dot_general | solution.py:280
  60.0 0.9 %fusion.7 = f32[3,1,24,256]{3,0,2,1:T(4,128)S(1)} fusion(f32[1,24,64,256]{3,2,1,0:T(8,128)S(1)} %copy-done, f32[24,8,256]{2,1,0:T(8,128)S(1)} %get-tuple-element.9, f32[3,24,64]{2,1,0:T(8,128)S(1)} %fusion.10), kind=kOutput, calls=%fused_computation.5 | convolution fusion | flops 14174208 | bytes 1738752 | tf_op jit(solution)/shard_map/slki,rslk->rsli/dot_general | solution.py:302
  60.9 0.6 %copy.32 = f32[3,1,24,256]{3,2,1,0:T(8,128)} copy(f32[3,1,24,256]{3,0,2,1:T(4,128)S(1)} %fusion.7) | data formatting | bytes 147456 | tf_op jit(solution)/shard_map/add | solution.py:302
  (10 shorter events, 0.1 us)
Async XLA Ops:
  0.0 2.6 %copy-start = (f32[1,24,64,256]{3,2,1,0:T(8,128)S(1)}, f32[1,24,64,256]{3,2,1,0:T(8,128)}, u32[]{:S(2)}) copy-start(f32[1,24,64,256]{3,2,1,0:T(8,128)} %param.13) | copy-start | bytes 4718596
  0.0 5.4 %copy-start.5 = (f32[1,1,64,64]{3,2,1,0:T(8,128)S(1)}, f32[1,1,64,64]{3,2,1,0:T(8,128)}, u32[]{:S(2)}) copy-start(f32[1,1,64,64]{3,2,1,0:T(8,128)} %param.15) | copy-start | bytes 49156
  0.0 4.8 %copy-start.1 = (f32[1,24,64,64]{3,2,1,0:T(8,128)S(1)}, f32[1,24,64,64]{3,2,1,0:T(8,128)}, u32[]{:S(2)}) copy-start(f32[1,24,64,64]{3,2,1,0:T(8,128)} %param.14) | copy-start | bytes 1179652
  0.0 5.6 %copy-start.6 = (f32[1,24,256]{2,1,0:T(8,128)S(1)}, f32[1,24,256]{2,1,0:T(8,128)}, u32[]{:S(2)}) copy-start(f32[1,24,256]{2,1,0:T(8,128)} %param.12) | copy-start | bytes 73732
  0.0 5.6 %copy-start.4 = (f32[3,1,24,256]{3,2,1,0:T(8,128)S(1)}, f32[3,1,24,256]{3,2,1,0:T(8,128)}, u32[]{:S(2)}) copy-start(f32[3,1,24,256]{3,2,1,0:T(8,128)} %param.10) | copy-start | bytes 221188
  0.0 5.6 %copy-start.7 = (f32[3,1,24,256]{3,2,1,0:T(8,128)S(1)}, f32[3,1,24,256]{3,2,1,0:T(8,128)}, u32[]{:S(2)}) copy-start(f32[3,1,24,256]{3,2,1,0:T(8,128)} %param.11) | copy-start | bytes 221188
  4.8 49.7 %copy-start.3 = (f32[1,16,64,64]{3,2,1,0:T(8,128)S(1)}, f32[1,16,64,64]{3,2,1,0:T(8,128)}, u32[]{:S(2)}) copy-start(f32[1,16,64,64]{3,2,1,0:T(8,128)} %param.18) | copy-start | bytes 786436
  57.7 1.2 %copy-start.2 = (f32[1,30,64,64]{3,2,1,0:T(8,128)S(1)}, f32[1,30,64,64]{3,2,1,0:T(8,128)}, u32[]{:S(2)}) copy-start(f32[1,30,64,64]{3,2,1,0:T(8,128)} %param.16) | copy-start | bytes 1474564
where the time goes:
time: 61.8 us; the launch traced here: 61.6 us
  Pallas kernels  48.5 us (78%)
  matrix products  7.66 us (12%)
  local copies, waits for them, and re-layouts  3.35 us (5%)
  other arithmetic  1.88 us (3%)
    pallas_call x1, Pallas kernels, exchange(): pl.pallas_call(exchange_kernel, out_shape=(jax.ShapeDtypeStruct((leaves,...  48.5 us
    dot_general x1, matrix products, body(): jnp.einsum('slki,rsli->rslk', leaf_basis, values, precision=HIGHEST_ACCUR...  2.26 us
    dot_general x1, matrix products, body(): jnp.einsum('slqk,rsk->rslq', transfer, slab_local_coefs, precision=HIGHES...  1.94 us

commit v1 on v0

v1 whole, which is shorter than its diff:
```python
import functools

import jax
import jax.numpy as jnp
from jax import lax
from jax.experimental import pallas as pl
from jax.experimental.pallas import tpu as pltpu
from jax.sharding import PartitionSpec as P

REACH = 6


SHARPNESS = 2.0
KERNEL_SCALE = 0.125
HIGHEST_ACCURACY = lax.Precision.HIGHEST


LOG2E = 1.4426950408889634


def halves(x):
    high = x.astype(jnp.bfloat16)
    return high, (x - high.astype(jnp.float32)).astype(jnp.bfloat16)


def near_steps(cells_ref, stiff_ref, near_ref, work):
    feature_ref, low_ref, high_ref, weight_ref, point_ref, factor_ref, *tiles = work
    leaves, size = stiff_ref.shape
    slots = cells_ref.shape[2]
    group = 16

    def prepare(a):
        for g in range(slots // group):
            rows = pl.ds(group * g, group)
            y0 = cells_ref[a, 0, rows] + (a - 1.0)
            y1, y2 = cells_ref[a, 1, rows], cells_ref[a, 2, rows]
            norm = (-SHARPNESS * LOG2E) * (y0 * y0 + y1 * y1 + y2 * y2)
            coarse = norm.astype(jnp.bfloat16).astype(jnp.float32)
            stacked = jnp.concatenate([y0, y1, y2, coarse, y0, y1, y2, norm - coarse], 0).T
            feature_ref[a, g] = jnp.concatenate(halves(stacked), 1)
        for k in range(2):
            lanes = pl.ds(128 * k, 128)
            wide = (low_ref, high_ref)[k]
            for g in range(slots // 8):
                for r in range(3):
                    w = cells_ref[a, 3 + r, pl.ds(8 * g, 8), lanes]
                    rounded = w.astype(jnp.bfloat16).astype(jnp.float32)
                    wide[pl.ds(128 * g + r, 8, stride=16)] = rounded
                    wide[pl.ds(128 * g + 8 + r, 8, stride=16)] = w - rounded
            weight_ref[a, :, lanes] = wide[...].astype(jnp.bfloat16)

    def targets():
        low_ref[...] = jnp.zeros_like(low_ref)
        high_ref[...] = jnp.zeros_like(high_ref)
        own = pl.ds(0, leaves)
        x0, x1, x2 = (cells_ref[1, d, own] for d in range(3))
        planes = [x0, x2] + [x1 - (b - 1.0) for b in range(3)]
        for k, z in enumerate(planes):
            z = z * (2 * SHARPNESS * LOG2E)
            rounded = z.astype(jnp.bfloat16).astype(jnp.float32)
            point_ref[2 * k] = rounded
            point_ref[2 * k + 1] = (z - rounded).astype(jnp.bfloat16).astype(jnp.float32)
        across = x0 * x0 + x2 * x2
        for b in range(3):
            z1 = planes[2 + b]
            factor_ref[b] = (
                KERNEL_SCALE * stiff_ref[...] * jnp.exp2((-SHARPNESS * LOG2E) * (across + z1 * z1))
            )

    row = lax.broadcasted_iota(jnp.int32, (group, size), 0)

    def slot_of(leaf):
        return jnp.where(leaf < 0, leaves, jnp.where(leaf >= leaves, leaves + 1, leaf))

    def right_side(t, b):
        slot = slot_of(t + (b - 1))
        chosen = row == lax.rem(slot, group)

        def block(k):
            return jnp.where(chosen, point_ref[k, pl.ds(t, 1)], 0.0).astype(jnp.bfloat16)

        one = jnp.where(chosen, 1.0, 0.0).astype(jnp.bfloat16)
        k = 4 + 2 * b
        blocks = [block(0), block(k), block(2), one, block(1), block(k + 1), block(3), one]
        return slot // group, jnp.concatenate(blocks + blocks, 0)

    def run(sources, first, together):
        count = len(sources)

        def fill(t, i, b, into):
            g, right = right_side(t, b)
            for n, a in enumerate(sources):
                power = jnp.dot(feature_ref[a, g], right, preferred_element_type=jnp.float32)
                high, low = halves(jnp.exp2(power))
                k = (i * 3 + b) * count + n
                into[0][k] = high
                into[1][k] = low

        def use(t, i, b, taken, total):
            slot = slot_of(t + (b - 1))
            got = None
            for n, a in enumerate(sources):
                weight = weight_ref[a, pl.ds(pl.multiple_of(slot * 16, 16), 16)]
                k = (i * 3 + b) * count + n
                for part in taken:
                    term = jnp.dot(weight, part[k], preferred_element_type=jnp.float32)
                    got = term if got is None else got + term
            term = (got[:8] + got[8:]) * factor_ref[b, pl.ds(t, 1)]
            return term if total is None else total + term

        def half(ahead, now, into, taken):
            for i in range(together):
                total = None
                for b in range(3):
                    fill(jnp.minimum(ahead + i, leaves - 1), i, b, into)
                    total = use(now + i, i, b, taken, total)
                for r in range(3):
                    line = total[r : r + 1]
                    at = pl.ds(now + i, 1)
                    near_ref[r, at] = line if first else near_ref[r, at] + line

        even, odd = tiles[:2], tiles[2:]
        for i in range(together):
            for b in range(3):
                fill(i, i, b, even)

        def step(k, carry):
            t = k * 2 * together
            half(t + together, t, odd, even)
            half(t + 2 * together, t + together, even, odd)
            return carry

        lax.fori_loop(0, leaves // (2 * together), step, 0)

    return prepare, targets, run


def far_offsets():
    ahead = list(range(2, REACH + 1))
    return ahead + [-step for step in ahead]


def exchange_kernel(
    cells_ref,
    edges_ref,
    stiff_ref,
    coefs_ref,
    ends_ref,
    share_ref,
    near_ref,
    windows_ref,
    rims_ref,
    shares_ref,
    padded_ref,
    brims_ref,
    send_sem,
    recv_sem,
    share_send_sem,
    share_recv_sem,
    *work,
):
    sectors, slabs = lax.axis_size("blk"), lax.axis_size("along")
    sector, slab = lax.axis_index("blk"), lax.axis_index("along")
    leaves = cells_ref.shape[1]
    slots = padded_ref.shape[2]
    copies = []

    def send(source, target, around, along):
        k = len(copies)
        copy = pltpu.make_async_remote_copy(
            src_ref=source,
            dst_ref=target,
            send_sem=send_sem.at[k],
            recv_sem=recv_sem.at[k],
            device_id={
                "blk": lax.rem(sector + around + sectors, sectors),
                "along": lax.rem(slab + along + slabs, slabs),
            },
            device_id_type=pl.DeviceIdType.MESH,
        )
        copy.start()
        copies.append(copy)

    distant = sectors - 2 * REACH - 1

    def share_copy(k, row, column):
        return pltpu.make_async_remote_copy(
            src_ref=share_ref,
            dst_ref=shares_ref.at[row, column],
            send_sem=share_send_sem.at[k],
            recv_sem=share_recv_sem.at[k // slabs * slabs + column],
            device_id={
                "blk": lax.rem(sector + REACH + 1 + k // slabs, sectors),
                "along": lax.rem(k, slabs),
            },
            device_id_type=pl.DeviceIdType.MESH,
        )

    def share_start(k, carry):
        share_copy(k, sector, slab).start()
        return carry

    def share_wait(k, carry):
        came = lax.rem(sector + sectors - REACH - 1 - k // slabs, sectors)
        share_copy(k, sector, slab).wait_send()
        share_copy(k, came, lax.rem(k, slabs)).wait_recv()
        return carry

    for around in (0, -1, 1):
        send(edges_ref.at[1], brims_ref.at[1 - around, 0], around, 1)
        send(edges_ref.at[0], brims_ref.at[1 - around, 1], around, -1)
    for around in (-1, 1):
        send(cells_ref, padded_ref.at[1 - around, :, pl.ds(0, leaves)], around, 0)
    lax.fori_loop(0, distant * slabs, share_start, 0)
    for q, around in enumerate(far_offsets()):
        send(coefs_ref, windows_ref.at[q], -around, 0)
        send(ends_ref.at[1], rims_ref.at[q, 0], -around, 1)
        send(ends_ref.at[0], rims_ref.at[q, 1], -around, -1)
    prepare, targets, run = near_steps(padded_ref, stiff_ref, near_ref, work)
    padded_ref[1, :, pl.ds(0, leaves)] = cells_ref[...]
    spare = jnp.zeros((slots - leaves, cells_ref.shape[2]), jnp.float32)
    at = lax.broadcasted_iota(jnp.int32, spare.shape, 0)

    def close(a):
        for d in range(6):
            before, after = brims_ref[a, 0, d : d + 1], brims_ref[a, 1, d : d + 1]
            before = jnp.where(slab == 0, 0.0, before)
            after = jnp.where(slab == slabs - 1, 0.0, after)
            padded_ref[a, d, pl.ds(leaves, slots - leaves)] = jnp.where(
                at == 0, before, jnp.where(at == 1, after, spare)
            )

    targets()
    for copy in copies[:2]:
        copy.wait()
    close(1)
    prepare(1)
    run((1,), True, 2)
    for copy in copies[2:8]:
        copy.wait()
    close(0)
    close(2)
    prepare(0)
    prepare(2)
    run((0, 2), False, 2)
    for copy in copies[8:]:
        copy.wait()
    lax.fori_loop(0, distant * slabs, share_wait, 0)

    @pl.when(slab == 0)
    def _():
        rims_ref[:, 0] = jnp.zeros_like(rims_ref[:, 0])

    @pl.when(slab == slabs - 1)
    def _():
        rims_ref[:, 1] = jnp.zeros_like(rims_ref[:, 1])


def exchange(cells, edges, stiffness, coefs, ends, share):
    sectors, slabs = lax.axis_size("blk"), lax.axis_size("along")
    _, leaves, size = cells.shape
    slots = -(-(leaves + 2) // 16) * 16
    far = 2 * (REACH - 1)
    links = 8 + 3 * far
    pairs = (sectors - 2 * REACH - 1) * slabs
    vmem = pl.BlockSpec(memory_space=pltpu.VMEM)
    return pl.pallas_call(
        exchange_kernel,
        out_shape=(
            jax.ShapeDtypeStruct((3, leaves, size), jnp.float32),
            jax.ShapeDtypeStruct((far, *coefs.shape), jnp.float32),
            jax.ShapeDtypeStruct((far, *ends.shape), jnp.float32),
            jax.ShapeDtypeStruct((sectors, slabs, *share.shape), jnp.float32),
        ),
        in_specs=[vmem] * 6,
        out_specs=(vmem,) * 4,
        scratch_shapes=[
            pltpu.VMEM((3, 6, slots, size), jnp.float32),
            pltpu.VMEM((3, 2, 8, size), jnp.float32),
            pltpu.SemaphoreType.DMA((links,)),
            pltpu.SemaphoreType.DMA((links,)),
            pltpu.SemaphoreType.DMA((pairs,)),
            pltpu.SemaphoreType.DMA((pairs,)),
            pltpu.VMEM((3, slots // 16, size, 256), jnp.bfloat16),
            pltpu.VMEM((slots * 16, 128), jnp.float32),
            pltpu.VMEM((slots * 16, 128), jnp.float32),
            pltpu.VMEM((3, slots * 16, size), jnp.bfloat16),
            pltpu.VMEM((10, leaves, size), jnp.float32),
            pltpu.VMEM((3, leaves, size), jnp.float32),
            *[pltpu.VMEM((12, size, size), jnp.bfloat16)] * 4,
        ],
        compiler_params=pltpu.CompilerParams(
            has_side_effects=True, vmem_limit_bytes=40 * 1024 * 1024
        ),
    )(cells, edges, stiffness, coefs, ends, share)


def body(
    values,
    offsets,
    stiffness,
    leaf_basis,
    transfer,
    slab_transfer_matrices,
    leaf_coupling_matrices,
    leaf_admissible_mask,
    top_coupling,
    top_admissible,
):
    cells = jnp.concatenate([offsets - 0.5, stiffness[None] * values], 0)[:, 0]
    edges = jnp.stack([cells[:, 0], cells[:, -1]])
    edges = jnp.pad(edges, ((0, 0), (0, 2), (0, 0)))
    coefs = jnp.einsum("slki,rsli->rslk", leaf_basis, values, precision=HIGHEST_ACCURACY)
    slab_coefficient_rows = jnp.einsum(
        "slqk,rslq->rsk", transfer, coefs, precision=HIGHEST_ACCURACY
    )
    shared_portion = jnp.einsum(
        "oxz,eox->eoz",
        slab_transfer_matrices[:, 0],
        slab_coefficient_rows,
        precision=HIGHEST_ACCURACY,
    )
    by_leaf = coefs[:, 0].transpose(1, 0, 2)
    leaves, count, rank = by_leaf.shape
    width = -(-count * rank // 128) * 128
    lanes = -(-rank // 128) * 128
    flat = by_leaf.reshape(leaves, count * rank)
    ends = jnp.stack([by_leaf[0], by_leaf[-1]])
    near, windows, rims, shares = exchange(
        cells,
        edges,
        stiffness[0],
        jnp.pad(flat, ((0, 0), (0, width - count * rank))),
        jnp.pad(ends, ((0, 0), (0, 8 - count), (0, lanes - rank))),
        jnp.pad(shared_portion[:, 0], ((0, 8 - count), (0, lanes - rank))),
    )
    near = near[:, None]
    far = windows.shape[0]
    windows = windows[:, :, : count * rank].reshape(far, leaves, count, rank)
    rims = rims[:, :, :count, :rank]
    windows = jnp.concatenate([rims[:, :1], windows, rims[:, 1:]], 1)
    partners = jnp.stack([windows[:, b : b + leaves] for b in range(3)], 1)
    coupling = (
        leaf_coupling_matrices[0] * leaf_admissible_mask[0].astype(jnp.float32)[:, None, None]
    ).reshape(far, 3, rank, rank)
    far_leaf = jnp.einsum(
        "qbkz,qblrz->rlk", coupling, partners, precision=HIGHEST_ACCURACY
    )[:, None]
    sectors = lax.axis_size("blk")
    sector = lax.axis_index("blk")
    others = jnp.arange(sectors, dtype=jnp.int32)
    apart = (others - sector) % sectors
    distant = jnp.logical_and(apart > REACH, apart < sectors - REACH)
    allowed = jnp.where(distant, top_admissible[0].astype(jnp.float32), 0.0)
    shares = jnp.where(distant[:, None, None, None], shares, 0.0)
    every_sector = shares.sum(1)[:, :count, :rank].transpose(1, 0, 2)
    sector_local_coefs = jnp.einsum(
        "stkq,rtq->rsk",
        top_coupling * allowed[None, :, None, None],
        every_sector,
        precision=HIGHEST_ACCURACY,
    )
    slab_local_coefs = jnp.einsum(
        "baz,lbz->lba", slab_transfer_matrices[:, 0], sector_local_coefs, precision=HIGHEST_ACCURACY
    )
    leaf_down = jnp.einsum("slqk,rsk->rslq", transfer, slab_local_coefs, precision=HIGHEST_ACCURACY)
    leaf_local = far_leaf + leaf_down
    return near + jnp.einsum("slki,rslk->rsli", leaf_basis, leaf_local, precision=HIGHEST_ACCURACY)


def solution(mesh):
    return jax.shard_map(
        body,
        mesh=mesh,
        in_specs=(
            P(None, "blk", "along", None),
            P(None, "blk", "along", None),
            P("blk", "along", None),
            P("blk", "along", None, None),
            P("blk", "along", None, None),
            P("blk", "along", None, None),
            P("blk", None, None, None),
            P("blk", None),
            P("blk", None, None, None),
            P("blk", None),
        ),
        out_specs=P(None, "blk", "along", None),
        check_vma=False,
    )
```

time: 61.8 us -> 42.7 us (0.69)
  Pallas kernels: 48.5 us -> 30.2 us
  local copies, waits for them, and re-layouts: 3.35 us -> 1.92 us
  other arithmetic: 1.88 us -> 2.5 us
    pallas_call x1, Pallas kernels: 48.5 us -> 30.2 us  [exchange(): pl.pallas_call(exchange_kernel, out_shape=(jax.ShapeDtypeStruct((3, leave...]
    broadcast_in_dim x1 -> x0, local copies, waits for them, and re-layouts: 0.76 us -> none  [body(): stiffness[None] * values]
    add x0 -> x1, other arithmetic: none -> 0.66 us  [body(): near + jnp.einsum('slki,rslk->rsli', leaf_basis, leaf_local, precision=HI...]
    add x1 -> x0, local copies, waits for them, and re-layouts: 0.65 us -> none  [body(): near + jnp.einsum('slki,rslk->rsli', leaf_basis, leaf_local, precision=HI...]
where the time goes in v1:
time: 42.7 us; the launch traced here: 42.4 us
  Pallas kernels  30.2 us (71%)
  matrix products  7.65 us (18%)
  other arithmetic  2.5 us (6%)
  local copies, waits for them, and re-layouts  1.92 us (4%)
    pallas_call x1, Pallas kernels, exchange(): pl.pallas_call(exchange_kernel, out_shape=(jax.ShapeDtypeStruct((3, leave...  30.2 us
    dot_general x1, matrix products, body(): jnp.einsum('slki,rsli->rslk', leaf_basis, values, precision=HIGHEST_ACCUR...  2.27 us
    dot_general x1, matrix products, body(): jnp.einsum('slqk,rsk->rslq', transfer, slab_local_coefs, precision=HIGHES...  1.94 us
    dot_general x1, matrix products, body(): jnp.einsum('qbkz,qblrz->rlk', coupling, partners, precision=HIGHEST_ACCUR...  1.18 us
    unnamed x16, local copies, waits for them, and re-layouts  1.09 us
    dot_general x1, matrix products, body(): jnp.einsum('slki,rslk->rsli', leaf_basis, leaf_local, precision=HIGHEST_A...  0.86 us

profile of v1, /device:TPU:0, one launch (start us, length us, event | category | flops | bytes accessed | tf_op | source)
XLA Modules:
  0.0 42.4 jit_solution(6868109903304177438)
XLA Ops:
  0.0 0.0 copy-start
  0.0 0.0 copy-start.6
  0.0 0.0 copy-start.2
  0.0 0.0 copy-start.5
  0.0 0.0 copy-start.1
  0.0 0.0 copy-start.7
  0.0 0.8 %convert_reduce_fusion = f32[30]{0:T(128)S(1)} fusion(s32[1,30]{1,0:T(1,128)} %param.17), kind=kLoop, calls=%fused_computation.53 | loop fusion | flops 30 | bytes 240 | tf_op jit(solution)/shard_map/convert_element_type | solution.py:344
  0.9 0.7 %bitcast_select_fusion = f32[16]{0:T(128)S(1)} fusion(s32[1,16]{1,0:T(1,128)} %param.19, s32[]{:T(128)S(6)} %axis_index.15), kind=kLoop, calls=%fused_computation.52 | loop fusion | flops 272 | bytes 132 | tf_op jit(solution)/shard_map/jit(_where)/select_n | solution.py:354
  1.5 0.1 convert_element_type.29
  1.6 0.1 copy.33
  1.7 0.0 copy-done
  1.7 2.3 %fusion.2 = f32[24,3,64]{2,1,0:T(4,128)S(1)} fusion(f32[1,24,64,256]{3,2,1,0:T(8,128)S(1)} %copy-done, f32[3,24,256]{2,1,0:T(8,128)} %bitcast.85), kind=kOutput, calls=%fused_computation.2 | convolution fusion | flops 14155776 | bytes 1665024 | tf_op jit(solution)/shard_map/slki,rsli->rslk/dot_general | solution.py:313
  4.0 0.0 copy-done.2
  4.0 0.0 copy-start.4
  4.0 0.5 %convolution_bitcast_fusion.3 = f32[3,64]{1,0:T(4,128)S(1)} fusion(f32[1,24,64,64]{3,2,1,0:T(8,128)S(1)} %copy-done.2, f32[24,3,64]{2,1,0:T(4,128)S(1)} %fusion.2), kind=kOutput, calls=%fused_computation.8 | convolution fusion | flops 3538944 | bytes 412416 | tf_op jit(solution)/shard_map/slqk,rslq->rsk/dot_general | solution.py:314
  4.5 0.0 copy-done.6
  4.5 0.1 fusion.25
  4.7 0.1 reshape.109
  4.8 0.0 copy-done.5
  4.8 0.0 copy-done.1
  4.8 0.0 copy-done.7
  4.8 0.1 copy_multiply_fusion.2
  5.0 0.1 copy.27.cells_ref
  5.1 30.2 %shard_map.100 = (f32[3,24,256]{2,1,0:T(8,128)S(1)}, f32[10,24,256]{2,1,0:T(8,128)S(1)}, f32[10,2,8,128]{3,2,1,0:T(8,128)S(1)}, f32[16,2,8,128]{3,2,1,0:T(8,128)S(1)}) custom-call(f32[6,24,256]{2,1,0:T(8,128)S(1)} %copy.27.cells_ref, f32[2,8,256]{2,1,0:T(8,128)S(1)} %select_maximum_fusion.edges_ref, f32[24,256]{1,0:T(8,128)S(1)} %bitcast.83, ...), custom_call_target="tpu_custom_call" | custom-call | tf_op jit(solution)/shard_map/pallas_call | solution.py:267
  35.3 0.1 select_reduce_fusion
  35.4 0.0 copy-done.4
  35.4 0.6 %convolution_bitcast_fusion.1 = f32[3,64]{1,0:T(4,128)S(1)} fusion(f32[1,16,64,64]{3,2,1,0:T(8,128)S(1)} %copy-done.4, f32[16]{0:T(128)S(1)} %bitcast_select_fusion, f32[16,8,128]{2,1,0:T(8,128)S(1)} %select_reduce_fusion), kind=kOutput, calls=%fused_computation.6 | convolution fusion | flops 2424832 | bytes 558336 | tf_op jit(solution)/shard_map/stkq,rtq->rsk/dot_general | solution.py:357
  36.0 0.2 convolution_bitcast_fusion.2
  36.1 1.9 %fusion.11 = f32[3,24,64]{2,0,1:T(4,128)S(1)} fusion(f32[3,64,1]{1,0,2:T(4,128)S(1)} %convolution_bitcast_fusion.2, f32[1,24,64,64]{3,2,1,0:T(8,128)S(1)} %copy-done.2), kind=kOutput, calls=%fused_computation.16 | convolution fusion | flops 3538944 | bytes 412416 | tf_op jit(solution)/shard_map/slqk,rsk->rslq/dot_general | solution.py:366
  38.1 0.2 stack_reshape.3
  38.3 0.2 reshape.113
  38.5 0.0 copy-start.3
  38.6 0.1 fusion.18
  38.7 1.1 %copy-done.3 = f32[1,30,64,64]{3,2,1,0:T(8,128)S(1)} copy-done((f32[1,30,64,64]{3,2,1,0:T(8,128)S(1)}, f32[1,30,64,64]{3,2,1,0:T(8,128)}, u32[]{:S(2)}) %copy-start.3) | copy-done | bytes 491544
  39.7 1.2 %fusion.4 = f32[3,24,64]{2,1,0:T(8,128)S(1)} fusion(f32[10,1,24,3,64]{4,2,0,1,3:T(8,128)S(1)} %get-tuple-element.14, f32[10,1,24,3,64]{4,2,0,1,3:T(8,128)S(1)} %copy.32, f32[10,1,24,3,64]{4,2,0,1,3:T(8,128)S(1)} %get-tuple-element.13, f32[10,3,64,64]{3,2,1,0:T(8,128)S(1)} %bitcast.84, f32[10,3]{0,1:T(4,128)S(1)} %copy.33, f32[3,24,64]{2,0,1:T(4,128)S(1)} %fusion.11), kind=kOutput, calls=%fused_computation.5 | convolution fusion | flops 106572288 | bytes 1081464 | tf_op jit(solution)/shard_map/qbkz,qblrz->rlk/dot_general | solution.py:346
  40.9 0.9 %fusion = f32[24,3,256]{2,1,0:T(4,128)S(1)} fusion(f32[1,24,64,256]{3,2,1,0:T(8,128)S(1)} %copy-done, f32[3,24,64]{2,1,0:T(8,128)S(1)} %fusion.4), kind=kOutput, calls=%fused_computation | convolution fusion | flops 14155776 | bytes 1665024 | tf_op jit(solution)/shard_map/slki,rslk->rsli/dot_general | solution.py:368
  41.8 0.7 %fusion.21 = f32[3,1,24,256]{3,2,1,0:T(8,128)} fusion(f32[3,24,256]{2,1,0:T(8,128)S(1)} %get-tuple-element.9, f32[24,3,256]{2,1,0:T(4,128)S(1)} %fusion), kind=kLoop, calls=%fused_computation.33 | loop fusion | flops 18432 | bytes 221184 | tf_op jit(solution)/shard_map/add | solution.py:368
  (13 shorter events, 0.2 us)
Async XLA Ops:
  0.0 1.7 %copy-start = (f32[1,24,64,256]{3,2,1,0:T(8,128)S(1)}, f32[1,24,64,256]{3,2,1,0:T(8,128)}, u32[]{:S(2)}) copy-start(f32[1,24,64,256]{3,2,1,0:T(8,128)} %param.13) | copy-start | bytes 4718596
  0.0 4.5 %copy-start.6 = (f32[1,1,64,64]{3,2,1,0:T(8,128)S(1)}, f32[1,1,64,64]{3,2,1,0:T(8,128)}, u32[]{:S(2)}) copy-start(f32[1,1,64,64]{3,2,1,0:T(8,128)} %param.15) | copy-start | bytes 49156
  0.0 4.0 %copy-start.2 = (f32[1,24,64,64]{3,2,1,0:T(8,128)S(1)}, f32[1,24,64,64]{3,2,1,0:T(8,128)}, u32[]{:S(2)}) copy-start(f32[1,24,64,64]{3,2,1,0:T(8,128)} %param.14) | copy-start | bytes 1179652
  0.0 4.8 %copy-start.5 = (f32[3,1,24,256]{3,2,1,0:T(8,128)S(1)}, f32[3,1,24,256]{3,2,1,0:T(8,128)}, u32[]{:S(2)}) copy-start(f32[3,1,24,256]{3,2,1,0:T(8,128)} %param.10) | copy-start | bytes 221188
  0.0 4.8 %copy-start.1 = (f32[1,24,256]{2,1,0:T(8,128)S(1)}, f32[1,24,256]{2,1,0:T(8,128)}, u32[]{:S(2)}) copy-start(f32[1,24,256]{2,1,0:T(8,128)} %param.12) | copy-start | bytes 73732
  0.0 4.8 %copy-start.7 = (f32[3,1,24,256]{3,2,1,0:T(8,128)S(1)}, f32[3,1,24,256]{3,2,1,0:T(8,128)}, u32[]{:S(2)}) copy-start(f32[3,1,24,256]{3,2,1,0:T(8,128)} %param.11) | copy-start | bytes 221188
  4.0 31.4 %copy-start.4 = (f32[1,16,64,64]{3,2,1,0:T(8,128)S(1)}, f32[1,16,64,64]{3,2,1,0:T(8,128)}, u32[]{:S(2)}) copy-start(f32[1,16,64,64]{3,2,1,0:T(8,128)} %param.18) | copy-start | bytes 786436
  38.5 1.2 %copy-start.3 = (f32[1,30,64,64]{3,2,1,0:T(8,128)S(1)}, f32[1,30,64,64]{3,2,1,0:T(8,128)}, u32[]{:S(2)}) copy-start(f32[1,30,64,64]{3,2,1,0:T(8,128)} %param.16) | copy-start | bytes 1474564

commit v2 on v1

--- a/solution.py
+++ b/solution.py
@@ -1,5 +1,3 @@
-import functools
-
 import jax
 import jax.numpy as jnp
 from jax import lax
@@ -12,7 +10,6 @@
 
 SHARPNESS = 2.0
 KERNEL_SCALE = 0.125
-HIGHEST_ACCURACY = lax.Precision.HIGHEST
 
 
 LOG2E = 1.4426950408889634
@@ -140,19 +137,44 @@
     return ahead + [-step for step in ahead]
 
 
+def stack_halves(x):
+    rounded = x.astype(jnp.bfloat16).astype(jnp.float32)
+    return jnp.concatenate([rounded, x - rounded], 0).astype(jnp.bfloat16)
+
+
+def split_product(left, right, transposed):
+    dims = (((1,), (1 if transposed else 0,)), ((), ()))
+    high, low = halves(right)
+    return lax.dot_general(
+        left, high, dims, preferred_element_type=jnp.float32
+    ) + lax.dot_general(left, low, dims, preferred_element_type=jnp.float32)
+
+
+def fold(x):
+    half = x.shape[0] // 2
+    return x[:half] + x[half:]
+
+
 def exchange_kernel(
     cells_ref,
     edges_ref,
     stiff_ref,
-    coefs_ref,
-    ends_ref,
-    share_ref,
-    near_ref,
-    windows_ref,
-    rims_ref,
-    shares_ref,
+    values_ref,
+    basis_ref,
+    transfer_ref,
+    slab_ref,
+    coupling_ref,
+    mask_ref,
+    top_ref,
+    listed_ref,
+    out_ref,
     padded_ref,
     brims_ref,
+    coefs_ref,
+    windows_ref,
+    share_ref,
+    shares_ref,
+    far_ref,
     send_sem,
     recv_sem,
     share_send_sem,
@@ -163,6 +185,8 @@
     sector, slab = lax.axis_index("blk"), lax.axis_index("along")
     leaves = cells_ref.shape[1]
     slots = padded_ref.shape[2]
+    count = values_ref.shape[0]
+    rank = basis_ref.shape[1]
     copies = []
 
     def send(source, target, around, along):
@@ -211,12 +235,54 @@
         send(edges_ref.at[0], brims_ref.at[1 - around, 1], around, -1)
     for around in (-1, 1):
         send(cells_ref, padded_ref.at[1 - around, :, pl.ds(0, leaves)], around, 0)
+
+    lane = lax.broadcasted_iota(jnp.int32, (rank, 128), 1)
+
+    def up(l, carry):
+        columns, sums = carry
+        basis, link = basis_ref[l], transfer_ref[l]
+        new_columns, new_sums = [], []
+        for r in range(count):
+            terms = basis * values_ref[r, pl.ds(l, 1)]
+            partial = terms[:, :128]
+            for k in range(1, terms.shape[1] // 128):
+                partial = partial + terms[:, 128 * k : 128 * k + 128]
+            column = jnp.sum(partial, axis=1, keepdims=True)
+            new_columns.append(jnp.where(lane == l, column, columns[r]))
+            new_sums.append(sums[r] + link * column)
+        return tuple(new_columns), tuple(new_sums)
+
+    columns, sums = lax.fori_loop(
+        0,
+        leaves,
+        up,
+        (
+            (jnp.zeros((rank, 128), jnp.float32),) * count,
+            (jnp.zeros((rank, rank), jnp.float32),) * count,
+        ),
+        unroll=2,
+    )
+    rows = [column.T[:leaves] for column in columns]
+    width = coefs_ref.shape[1]
+    rows.append(jnp.zeros((leaves, width - count * rank), jnp.float32))
+    coefs_ref[...] = jnp.concatenate(rows, 1)
+    slab_rows = jnp.concatenate(
+        [jnp.sum(x, axis=0, keepdims=True) for x in sums]
+        + [jnp.zeros((8 - count, rank), jnp.float32)],
+        0,
+    )
+    portion = fold(split_product(stack_halves(slab_rows), slab_ref[...], False))
+    share_ref[...] = jnp.concatenate(
+        [portion, jnp.zeros((8, share_ref.shape[1] - rank), jnp.float32)], 1
+    )
+    offsets = far_offsets()
+    for q, around in enumerate(offsets):
+        send(coefs_ref, windows_ref.at[q, pl.ds(8, leaves)], -around, 0)
+        send(coefs_ref.at[pl.ds(leaves - 8, 8)], windows_ref.at[q, pl.ds(0, 8)], -around, 1)
+        send(coefs_ref.at[pl.ds(0, 8)], windows_ref.at[q, pl.ds(leaves + 8, 8)], -around, -1)
     lax.fori_loop(0, distant * slabs, share_start, 0)
-    for q, around in enumerate(far_offsets()):
-        send(coefs_ref, windows_ref.at[q], -around, 0)
-        send(ends_ref.at[1], rims_ref.at[q, 0], -around, 1)
-        send(ends_ref.at[0], rims_ref.at[q, 1], -around, -1)
-    prepare, targets, run = near_steps(padded_ref, stiff_ref, near_ref, work)
+
+    prepare, targets, run = near_steps(padded_ref, stiff_ref, out_ref, work)
     padded_ref[1, :, pl.ds(0, leaves)] = cells_ref[...]
     spare = jnp.zeros((slots - leaves, cells_ref.shape[2]), jnp.float32)
     at = lax.broadcasted_iota(jnp.int32, spare.shape, 0)
@@ -249,34 +315,78 @@
 
     @pl.when(slab == 0)
     def _():
-        rims_ref[:, 0] = jnp.zeros_like(rims_ref[:, 0])
+        windows_ref[:, pl.ds(0, 8)] = jnp.zeros_like(windows_ref[:, pl.ds(0, 8)])
 
     @pl.when(slab == slabs - 1)
     def _():
-        rims_ref[:, 1] = jnp.zeros_like(rims_ref[:, 1])
-
-
-def exchange(cells, edges, stiffness, coefs, ends, share):
+        windows_ref[:, pl.ds(leaves + 8, 8)] = jnp.zeros_like(windows_ref[:, pl.ds(0, 8)])
+
+    total = None
+    for q in range(len(offsets)):
+        left, right = [], []
+        for b in range(3):
+            window = windows_ref[q, pl.ds(7 + b, leaves)]
+            left.append(
+                jnp.concatenate([window[:, rank * r : rank * r + rank] for r in range(count)], 0)
+            )
+            right.append(coupling_ref[3 * q + b] * mask_ref[0, 3 * q + b].astype(jnp.float32))
+        term = split_product(
+            stack_halves(jnp.concatenate(left, 1)), jnp.concatenate(right, 1), True
+        )
+        total = term if total is None else total + term
+    far_ref[pl.ds(0, count * leaves)] = jnp.concatenate(
+        [fold(total), jnp.zeros((count * leaves, far_ref.shape[1] - rank), jnp.float32)], 1
+    )
+
+    def across(k, carry):
+        other = lax.rem(sector + REACH + 1 + k, sectors)
+        held = shares_ref[other, 0]
+        for p in range(1, slabs):
+            held = held + shares_ref[other, p]
+        block = top_ref[other] * listed_ref[0, other].astype(jnp.float32)
+        return carry + fold(split_product(stack_halves(held[:, :rank]), block, True))
+
+    sector_local = lax.fori_loop(0, distant, across, jnp.zeros((8, rank), jnp.float32))
+    slab_local = fold(split_product(stack_halves(sector_local), slab_ref[...], True))
+    slab_left = stack_halves(slab_local)
+
+    def down(l, carry):
+        local = fold(split_product(slab_left, transfer_ref[l], True))
+        side = [far_ref[pl.ds(leaves * r + l, 1)][:, :rank] for r in range(count)]
+        local = local + jnp.concatenate(side + [jnp.zeros((8 - count, rank), jnp.float32)], 0)
+        spread = fold(split_product(stack_halves(local), basis_ref[l], False))
+        for r in range(count):
+            out_ref[r, pl.ds(l, 1)] = out_ref[r, pl.ds(l, 1)] + spread[r : r + 1]
+        return carry
+
+    lax.fori_loop(0, leaves, down, 0, unroll=8 if leaves % 8 == 0 else 1)
+
+
+def exchange(cells, edges, stiffness, values, basis, transfer, slab, coupling, mask, top, listed):
     sectors, slabs = lax.axis_size("blk"), lax.axis_size("along")
     _, leaves, size = cells.shape
+    count, rank = values.shape[0], basis.shape[1]
+    width = -(-count * rank // 128) * 128
+    lanes = -(-rank // 128) * 128
     slots = -(-(leaves + 2) // 16) * 16
     far = 2 * (REACH - 1)
     links = 8 + 3 * far
     pairs = (sectors - 2 * REACH - 1) * slabs
     vmem = pl.BlockSpec(memory_space=pltpu.VMEM)
+    smem = pl.BlockSpec(memory_space=pltpu.SMEM)
     return pl.pallas_call(
         exchange_kernel,
-        out_shape=(
-            jax.ShapeDtypeStruct((3, leaves, size), jnp.float32),
-            jax.ShapeDtypeStruct((far, *coefs.shape), jnp.float32),
-            jax.ShapeDtypeStruct((far, *ends.shape), jnp.float32),
-            jax.ShapeDtypeStruct((sectors, slabs, *share.shape), jnp.float32),
-        ),
-        in_specs=[vmem] * 6,
-        out_specs=(vmem,) * 4,
+        out_shape=jax.ShapeDtypeStruct((count, leaves, size), jnp.float32),
+        in_specs=[vmem] * 8 + [smem, vmem, smem],
+        out_specs=vmem,
         scratch_shapes=[
             pltpu.VMEM((3, 6, slots, size), jnp.float32),
             pltpu.VMEM((3, 2, 8, size), jnp.float32),
+            pltpu.VMEM((leaves, width), jnp.float32),
+            pltpu.VMEM((far, leaves + 16, width), jnp.float32),
+            pltpu.VMEM((8, lanes), jnp.float32),
+            pltpu.VMEM((sectors, slabs, 8, lanes), jnp.float32),
+            pltpu.VMEM((count * leaves, lanes), jnp.float32),
             pltpu.SemaphoreType.DMA((links,)),
             pltpu.SemaphoreType.DMA((links,)),
             pltpu.SemaphoreType.DMA((pairs,)),
@@ -292,7 +402,7 @@
         compiler_params=pltpu.CompilerParams(
             has_side_effects=True, vmem_limit_bytes=40 * 1024 * 1024
         ),
-    )(cells, edges, stiffness, coefs, ends, share)
+    )(cells, edges, stiffness, values, basis, transfer, slab, coupling, mask, top, listed)
 
 
 def body(
@@ -310,62 +420,20 @@
     cells = jnp.concatenate([offsets - 0.5, stiffness[None] * values], 0)[:, 0]
     edges = jnp.stack([cells[:, 0], cells[:, -1]])
     edges = jnp.pad(edges, ((0, 0), (0, 2), (0, 0)))
-    coefs = jnp.einsum("slki,rsli->rslk", leaf_basis, values, precision=HIGHEST_ACCURACY)
-    slab_coefficient_rows = jnp.einsum(
-        "slqk,rslq->rsk", transfer, coefs, precision=HIGHEST_ACCURACY
-    )
-    shared_portion = jnp.einsum(
-        "oxz,eox->eoz",
-        slab_transfer_matrices[:, 0],
-        slab_coefficient_rows,
-        precision=HIGHEST_ACCURACY,
-    )
-    by_leaf = coefs[:, 0].transpose(1, 0, 2)
-    leaves, count, rank = by_leaf.shape
-    width = -(-count * rank // 128) * 128
-    lanes = -(-rank // 128) * 128
-    flat = by_leaf.reshape(leaves, count * rank)
-    ends = jnp.stack([by_leaf[0], by_leaf[-1]])
-    near, windows, rims, shares = exchange(
+    product = exchange(
         cells,
         edges,
         stiffness[0],
-        jnp.pad(flat, ((0, 0), (0, width - count * rank))),
-        jnp.pad(ends, ((0, 0), (0, 8 - count), (0, lanes - rank))),
-        jnp.pad(shared_portion[:, 0], ((0, 8 - count), (0, lanes - rank))),
-    )
-    near = near[:, None]
-    far = windows.shape[0]
-    windows = windows[:, :, : count * rank].reshape(far, leaves, count, rank)
-    rims = rims[:, :, :count, :rank]
-    windows = jnp.concatenate([rims[:, :1], windows, rims[:, 1:]], 1)
-    partners = jnp.stack([windows[:, b : b + leaves] for b in range(3)], 1)
-    coupling = (
-        leaf_coupling_matrices[0] * leaf_admissible_mask[0].astype(jnp.float32)[:, None, None]
-    ).reshape(far, 3, rank, rank)
-    far_leaf = jnp.einsum(
-        "qbkz,qblrz->rlk", coupling, partners, precision=HIGHEST_ACCURACY
-    )[:, None]
-    sectors = lax.axis_size("blk")
-    sector = lax.axis_index("blk")
-    others = jnp.arange(sectors, dtype=jnp.int32)
-    apart = (others - sector) % sectors
-    distant = jnp.logical_and(apart > REACH, apart < sectors - REACH)
-    allowed = jnp.where(distant, top_admissible[0].astype(jnp.float32), 0.0)
-    shares = jnp.where(distant[:, None, None, None], shares, 0.0)
-    every_sector = shares.sum(1)[:, :count, :rank].transpose(1, 0, 2)
-    sector_local_coefs = jnp.einsum(
-        "stkq,rtq->rsk",
-        top_coupling * allowed[None, :, None, None],
-        every_sector,
-        precision=HIGHEST_ACCURACY,
-    )
-    slab_local_coefs = jnp.einsum(
-        "baz,lbz->lba", slab_transfer_matrices[:, 0], sector_local_coefs, precision=HIGHEST_ACCURACY
-    )
-    leaf_down = jnp.einsum("slqk,rsk->rslq", transfer, slab_local_coefs, precision=HIGHEST_ACCURACY)
-    leaf_local = far_leaf + leaf_down
-    return near + jnp.einsum("slki,rslk->rsli", leaf_basis, leaf_local, precision=HIGHEST_ACCURACY)
+        values[:, 0],
+        leaf_basis[0],
+        transfer[0],
+        slab_transfer_matrices[0, 0],
+        leaf_coupling_matrices[0],
+        leaf_admissible_mask,
+        top_coupling[0],
+        top_admissible,
+    )
+    return product[:, None]
 
 
 def solution(mesh):

time: 42.7 us -> 46 us (1.077)
  matrix products: 7.65 us -> 0 us
  Pallas kernels: 30.2 us -> 36.3 us
  local copies, waits for them, and re-layouts: 1.92 us -> 7.99 us
  other arithmetic: 2.5 us -> 1.17 us
    dot_general x8 -> x0, matrix products: 7.65 us -> none  [the longest x1 2.27 us: body(): jnp.einsum('slki,rsli->rslk', leaf_basis, values, precision=HIGHEST_ACCUR...]
    unnamed x16 -> x19, local copies, waits for them, and re-layouts: 1.09 us -> 7.94 us
    pallas_call x1, Pallas kernels: 30.2 us -> 36.3 us  [exchange(): pl.pallas_call(exchange_kernel, out_shape=jax.ShapeDtypeStruct((count, le...]
    mul x1, other arithmetic: 0.09 us -> 1.11 us  [body(): cells = jnp.concatenate([offsets - 0.5, stiffness[None] * values], 0)[:, 0]]
    convert_element_type x1 -> x0, other arithmetic: 0.82 us -> none  [body(): leaf_admissible_mask[0].astype(jnp.float32)[:, None, None]]
    select_n x1 -> x0, other arithmetic: 0.67 us -> none  [body(): allowed = jnp.where(distant, top_admissible[0].astype(jnp.float32), 0.0)]
    add x1 -> x0, other arithmetic: 0.66 us -> none  [body(): near + jnp.einsum('slki,rslk->rsli', leaf_basis, leaf_local, precision=HI...]
where the time goes in v2:
time: 46 us; the launch traced here: 45.5 us
  Pallas kernels  36.3 us (79%)
  local copies, waits for them, and re-layouts  7.99 us (17%)
  other arithmetic  1.17 us (3%)
    pallas_call x1, Pallas kernels, exchange(): pl.pallas_call(exchange_kernel, out_shape=jax.ShapeDtypeStruct((count, le...  36.3 us
    unnamed x19, local copies, waits for them, and re-layouts  7.94 us
    mul x1, other arithmetic, body(): cells = jnp.concatenate([offsets - 0.5, stiffness[None] * values], 0)[:, 0]  1.11 us

profile of v2, /device:TPU:0, one launch (start us, length us, event | category | flops | bytes accessed | tf_op | source)
XLA Modules:
  0.0 45.5 jit_solution(11204325443835961105)
XLA Ops:
  0.0 0.0 copy-start.1
  0.0 1.1 %copy_multiply_fusion = (f32[3,1,24,256]{3,0,2,1:T(4,128)S(1)}, f32[3,1,24,256]{3,0,2,1:T(4,128)S(1)}) fusion(f32[3,1,24,256]{3,2,1,0:T(8,128)} %param.10, f32[24,256]{1,0:T(8,128)} %bitcast.22, f32[3,1,24,256]{3,2,1,0:T(8,128)} %param.11), kind=kLoop, calls=%fused_computation.1 | loop fusion | flops 36864 | bytes 319488 | tf_op jit(solution)/shard_map/mul | solution.py:420
  1.2 0.1 copy.18.cells_ref
  1.3 0.0 copy-done.1
  1.3 0.0 copy-start
  1.3 1.4 %copy-done = f32[1,24,64,256]{3,2,1,0:T(8,128)S(1)} copy-done((f32[1,24,64,256]{3,2,1,0:T(8,128)S(1)}, f32[1,24,64,256]{3,2,1,0:T(8,128)}, u32[]{:S(2)}) %copy-start) | copy-done | bytes 1572888
  2.7 0.0 copy-start.2
  2.7 1.1 %copy-done.2 = f32[1,24,64,64]{3,2,1,0:T(8,128)S(1)} copy-done((f32[1,24,64,64]{3,2,1,0:T(8,128)S(1)}, f32[1,24,64,64]{3,2,1,0:T(8,128)}, u32[]{:S(2)}) %copy-start.2) | copy-done | bytes 393240
  3.8 0.0 copy-start.3
  3.8 1.0 %copy-done.3 = f32[1,16,64,64]{3,2,1,0:T(8,128)S(1)} copy-done((f32[1,16,64,64]{3,2,1,0:T(8,128)S(1)}, f32[1,16,64,64]{3,2,1,0:T(8,128)}, u32[]{:S(2)}) %copy-start.3) | copy-done | bytes 262168
  4.9 0.0 copy-start.4
  4.9 0.9 %copy-done.4 = f32[3,1,24,256]{3,2,1,0:T(8,128)S(1)} copy-done((f32[3,1,24,256]{3,2,1,0:T(8,128)S(1)}, f32[3,1,24,256]{3,2,1,0:T(8,128)}, u32[]{:S(2)}) %copy-start.4) | copy-done | bytes 73752
  5.8 0.0 copy-start.5
  5.8 0.7 %copy-done.5 = f32[1,24,256]{2,1,0:T(8,128)S(1)} copy-done((f32[1,24,256]{2,1,0:T(8,128)S(1)}, f32[1,24,256]{2,1,0:T(8,128)}, u32[]{:S(2)}) %copy-start.5) | copy-done | bytes 24600
  6.5 0.0 copy-start.6
  6.5 0.8 %copy-done.6 = f32[1,1,64,64]{3,2,1,0:T(8,128)S(1)} copy-done((f32[1,1,64,64]{3,2,1,0:T(8,128)S(1)}, f32[1,1,64,64]{3,2,1,0:T(8,128)}, u32[]{:S(2)}) %copy-start.6) | copy-done | bytes 16408
  7.3 0.0 copy-start.7
  7.3 0.7 %copy-done.7 = s32[1,30]{1,0:T(1,128)S(1)} copy-done((s32[1,30]{1,0:T(1,128)S(1)}, s32[1,30]{1,0:T(1,128)}, u32[]{:S(2)}) %copy-start.7) | copy-done | bytes 144
  7.9 0.0 copy-start.8
  7.9 0.7 %copy-done.8 = s32[1,16]{1,0:T(1,128)S(1)} copy-done((s32[1,16]{1,0:T(1,128)S(1)}, s32[1,16]{1,0:T(1,128)}, u32[]{:S(2)}) %copy-start.8) | copy-done | bytes 88
  8.6 36.3 %shard_map.100 = f32[3,24,256]{2,1,0:T(8,128)S(1)} custom-call(f32[6,24,256]{2,1,0:T(8,128)S(1)} %copy.18.cells_ref, f32[2,8,256]{2,1,0:T(8,128)S(1)} %select_maximum_fusion.edges_ref, f32[24,256]{1,0:T(8,128)S(1)} %bitcast.23, f32[3,24,256]{2,1,0:T(8,128)S(1)} %bitcast.21, f32[24,64,256]{2,1,0:T(8,128)S(1)} %bitcast.16, f32[24,64,64]{2,1,0:T(8,128)S(1)} %bitcast.18, ...), custom_call_target="tpu_custom_call" | custom-call | tf_op jit(solution)/shard_map/pallas_call | solution.py:377
  44.9 0.6 %copy.23 = f32[3,1,24,256]{3,2,1,0:T(8,128)} copy(f32[3,1,24,256]{3,2,1,0:T(8,128)S(1)} %bitcast.20) | data formatting | bytes 147456
  (3 shorter events, 0.1 us)
Async XLA Ops:
  0.0 1.3 %copy-start.1 = (f32[1,30,64,64]{3,2,1,0:T(8,128)S(1)}, f32[1,30,64,64]{3,2,1,0:T(8,128)}, u32[]{:S(2)}) copy-start(f32[1,30,64,64]{3,2,1,0:T(8,128)} %param.16) | copy-start | bytes 1474564
  1.3 1.4 %copy-start = (f32[1,24,64,256]{3,2,1,0:T(8,128)S(1)}, f32[1,24,64,256]{3,2,1,0:T(8,128)}, u32[]{:S(2)}) copy-start(f32[1,24,64,256]{3,2,1,0:T(8,128)} %param.13) | copy-start | bytes 4718596
  2.7 1.1 %copy-start.2 = (f32[1,24,64,64]{3,2,1,0:T(8,128)S(1)}, f32[1,24,64,64]{3,2,1,0:T(8,128)}, u32[]{:S(2)}) copy-start(f32[1,24,64,64]{3,2,1,0:T(8,128)} %param.14) | copy-start | bytes 1179652
  3.8 1.0 %copy-start.3 = (f32[1,16,64,64]{3,2,1,0:T(8,128)S(1)}, f32[1,16,64,64]{3,2,1,0:T(8,128)}, u32[]{:S(2)}) copy-start(f32[1,16,64,64]{3,2,1,0:T(8,128)} %param.18) | copy-start | bytes 786436
  4.9 0.9 %copy-start.4 = (f32[3,1,24,256]{3,2,1,0:T(8,128)S(1)}, f32[3,1,24,256]{3,2,1,0:T(8,128)}, u32[]{:S(2)}) copy-start(f32[3,1,24,256]{3,2,1,0:T(8,128)} %param.10) | copy-start | bytes 221188
  5.8 0.7 %copy-start.5 = (f32[1,24,256]{2,1,0:T(8,128)S(1)}, f32[1,24,256]{2,1,0:T(8,128)}, u32[]{:S(2)}) copy-start(f32[1,24,256]{2,1,0:T(8,128)} %param.12) | copy-start | bytes 73732
  6.5 0.8 %copy-start.6 = (f32[1,1,64,64]{3,2,1,0:T(8,128)S(1)}, f32[1,1,64,64]{3,2,1,0:T(8,128)}, u32[]{:S(2)}) copy-start(f32[1,1,64,64]{3,2,1,0:T(8,128)} %param.15) | copy-start | bytes 49156
  7.3 0.7 %copy-start.7 = (s32[1,30]{1,0:T(1,128)S(1)}, s32[1,30]{1,0:T(1,128)}, u32[]{:S(2)}) copy-start(s32[1,30]{1,0:T(1,128)} %mask_ref.1) | copy-start | bytes 364
  7.9 0.7 %copy-start.8 = (s32[1,16]{1,0:T(1,128)S(1)}, s32[1,16]{1,0:T(1,128)}, u32[]{:S(2)}) copy-start(s32[1,16]{1,0:T(1,128)} %listed_ref.1) | copy-start | bytes 196

commit v3 on v2

--- a/solution.py
+++ b/solution.py
@@ -156,18 +156,47 @@
 
 
 def exchange_kernel(
-    cells_ref,
-    edges_ref,
+    *refs,
+):
+    given, refs = refs[:8], refs[8:]
+    mask_ref, listed_ref, out_ref, *refs = refs
+    here, refs = refs[:8], refs[8:]
+    values_ref, offsets_ref, stiff_ref, basis_ref, transfer_ref = here[:5]
+    slab_ref, coupling_ref, top_ref = here[5:]
+    exchange_steps(
+        given,
+        here,
+        values_ref,
+        offsets_ref,
+        stiff_ref,
+        basis_ref,
+        transfer_ref,
+        slab_ref,
+        coupling_ref,
+        top_ref,
+        mask_ref,
+        listed_ref,
+        out_ref,
+        *refs,
+    )
+
+
+def exchange_steps(
+    given,
+    here,
+    values_ref,
+    offsets_ref,
     stiff_ref,
-    values_ref,
     basis_ref,
     transfer_ref,
     slab_ref,
     coupling_ref,
+    top_ref,
     mask_ref,
-    top_ref,
     listed_ref,
     out_ref,
+    cells_ref,
+    edges_ref,
     padded_ref,
     brims_ref,
     coefs_ref,
@@ -179,8 +208,15 @@
     recv_sem,
     share_send_sem,
     share_recv_sem,
+    load_sem,
     *work,
 ):
+    loads = [
+        pltpu.make_async_copy(source, target, load_sem.at[k])
+        for k, (source, target) in enumerate(zip(given, here))
+    ]
+    for load in loads:
+        load.start()
     sectors, slabs = lax.axis_size("blk"), lax.axis_size("along")
     sector, slab = lax.axis_index("blk"), lax.axis_index("along")
     leaves = cells_ref.shape[1]
@@ -230,11 +266,50 @@
         share_copy(k, came, lax.rem(k, slabs)).wait_recv()
         return carry
 
+    barrier = pltpu.get_barrier_semaphore()
+
+    def greet(around, along):
+        pl.semaphore_signal(
+            barrier,
+            inc=1,
+            device_id={
+                "blk": lax.rem(sector + around + sectors, sectors),
+                "along": lax.rem(slab + along + slabs, slabs),
+            },
+            device_id_type=pl.DeviceIdType.MESH,
+        )
+
+    greeted = 0
+    for around in (0, -1, 1, *far_offsets()):
+        for along in (-1, 0, 1):
+            if around or along:
+                greet(around, along)
+                greeted += 1
+
+    def greet_distant(k, carry):
+        greet(REACH + 1 + k // slabs, lax.rem(k, slabs))
+        return carry
+
+    lax.fori_loop(0, distant * slabs, greet_distant, 0)
+    for load in loads[:3]:
+        load.wait()
+    for d in range(3):
+        cells_ref[d] = offsets_ref[d] - 0.5
+        cells_ref[3 + d] = stiff_ref[...] * values_ref[d]
+    for d in range(6):
+        edges_ref[0, pl.ds(d, 1)] = cells_ref[d, pl.ds(0, 1)]
+        edges_ref[1, pl.ds(d, 1)] = cells_ref[d, pl.ds(leaves - 1, 1)]
+    for k in range(2):
+        edges_ref[k, pl.ds(6, 2)] = jnp.zeros((2, edges_ref.shape[2]), jnp.float32)
+    pl.semaphore_wait(barrier, greeted + distant * slabs)
     for around in (0, -1, 1):
         send(edges_ref.at[1], brims_ref.at[1 - around, 0], around, 1)
         send(edges_ref.at[0], brims_ref.at[1 - around, 1], around, -1)
     for around in (-1, 1):
         send(cells_ref, padded_ref.at[1 - around, :, pl.ds(0, leaves)], around, 0)
+
+    for load in loads[3:]:
+        load.wait()
 
     lane = lax.broadcasted_iota(jnp.int32, (rank, 128), 1)
 
@@ -362,24 +437,27 @@
     lax.fori_loop(0, leaves, down, 0, unroll=8 if leaves % 8 == 0 else 1)
 
 
-def exchange(cells, edges, stiffness, values, basis, transfer, slab, coupling, mask, top, listed):
+def exchange(arrays, mask, listed):
     sectors, slabs = lax.axis_size("blk"), lax.axis_size("along")
-    _, leaves, size = cells.shape
-    count, rank = values.shape[0], basis.shape[1]
+    count, leaves, size = arrays[0].shape
+    rank = arrays[3].shape[1]
     width = -(-count * rank // 128) * 128
     lanes = -(-rank // 128) * 128
     slots = -(-(leaves + 2) // 16) * 16
     far = 2 * (REACH - 1)
     links = 8 + 3 * far
     pairs = (sectors - 2 * REACH - 1) * slabs
-    vmem = pl.BlockSpec(memory_space=pltpu.VMEM)
+    hbm = pl.BlockSpec(memory_space=pltpu.HBM)
     smem = pl.BlockSpec(memory_space=pltpu.SMEM)
     return pl.pallas_call(
         exchange_kernel,
         out_shape=jax.ShapeDtypeStruct((count, leaves, size), jnp.float32),
-        in_specs=[vmem] * 8 + [smem, vmem, smem],
-        out_specs=vmem,
+        in_specs=[hbm] * len(arrays) + [smem] * 2,
+        out_specs=pl.BlockSpec(memory_space=pltpu.VMEM),
         scratch_shapes=[
+            *[pltpu.VMEM(x.shape, x.dtype) for x in arrays],
+            pltpu.VMEM((6, leaves, size), jnp.float32),
+            pltpu.VMEM((2, 8, size), jnp.float32),
             pltpu.VMEM((3, 6, slots, size), jnp.float32),
             pltpu.VMEM((3, 2, 8, size), jnp.float32),
             pltpu.VMEM((leaves, width), jnp.float32),
@@ -391,6 +469,7 @@
             pltpu.SemaphoreType.DMA((links,)),
             pltpu.SemaphoreType.DMA((pairs,)),
             pltpu.SemaphoreType.DMA((pairs,)),
+            pltpu.SemaphoreType.DMA((len(arrays),)),
             pltpu.VMEM((3, slots // 16, size, 256), jnp.bfloat16),
             pltpu.VMEM((slots * 16, 128), jnp.float32),
             pltpu.VMEM((slots * 16, 128), jnp.float32),
@@ -400,9 +479,9 @@
             *[pltpu.VMEM((12, size, size), jnp.bfloat16)] * 4,
         ],
         compiler_params=pltpu.CompilerParams(
-            has_side_effects=True, vmem_limit_bytes=40 * 1024 * 1024
+            collective_id=0, has_side_effects=True, vmem_limit_bytes=60 * 1024 * 1024
         ),
-    )(cells, edges, stiffness, values, basis, transfer, slab, coupling, mask, top, listed)
+    )(*arrays, mask, listed)
 
 
 def body(
@@ -417,23 +496,18 @@
     top_coupling,
     top_admissible,
 ):
-    cells = jnp.concatenate([offsets - 0.5, stiffness[None] * values], 0)[:, 0]
-    edges = jnp.stack([cells[:, 0], cells[:, -1]])
-    edges = jnp.pad(edges, ((0, 0), (0, 2), (0, 0)))
-    product = exchange(
-        cells,
-        edges,
+    arrays = (
+        values[:, 0],
+        offsets[:, 0],
         stiffness[0],
-        values[:, 0],
         leaf_basis[0],
         transfer[0],
         slab_transfer_matrices[0, 0],
         leaf_coupling_matrices[0],
-        leaf_admissible_mask,
         top_coupling[0],
-        top_admissible,
-    )
-    return product[:, None]
+    )
+    arrays = tuple(pltpu.with_memory_space_constraint(x, pltpu.HBM) for x in arrays)
+    return exchange(arrays, leaf_admissible_mask, top_admissible)[:, None]
 
 
 def solution(mesh):

time: 46 us -> 37.8 us (0.82)
  local copies, waits for them, and re-layouts: 7.99 us -> 1.52 us
  other arithmetic: 1.17 us -> 0 us
    unnamed x19 -> x1, local copies, waits for them, and re-layouts: 7.94 us -> 1.52 us
    mul x1 -> x0, other arithmetic: 1.11 us -> none  [body(): cells = jnp.concatenate([offsets - 0.5, stiffness[None] * values], 0)[:, 0]]
where the time goes in v3:
time: 37.8 us; the launch traced here: 37.7 us
  Pallas kernels  36.1 us (96%)
  local copies, waits for them, and re-layouts  1.52 us (4%)
    pallas_call x1, Pallas kernels, exchange(): pl.pallas_call(exchange_kernel, out_shape=jax.ShapeDtypeStruct((count, le...  36.1 us
    unnamed x1, local copies, waits for them, and re-layouts  1.52 us

profile of v3, /device:TPU:0, one launch (start us, length us, event | category | flops | bytes accessed | tf_op | source)
XLA Modules:
  0.0 37.7 jit_solution(9078906735624786858)
XLA Ops:
  0.0 36.1 %shard_map.100 = f32[3,24,256]{2,1,0:T(8,128)} custom-call(f32[3,24,256]{2,1,0:T(8,128)} %bitcast.16, f32[3,24,256]{2,1,0:T(8,128)} %bitcast.17, f32[24,256]{1,0:T(8,128)} %bitcast.19, f32[24,64,256]{2,1,0:T(8,128)} %bitcast.11, f32[24,64,64]{2,1,0:T(8,128)} %bitcast.13, f32[64,64]{1,0:T(8,128)} %bitcast.18, f32[30,64,64]{2,1,0:T(8,128)} %bitcast.12, ...), custom_call_target="tpu_custom_call" | custom-call | tf_op jit(solution)/shard_map/pallas_call | solution.py:452
  36.1 1.5 %copy.13 = f32[3,1,24,256]{3,2,1,0:T(8,128)} copy(f32[3,1,24,256]{3,2,1,0:T(8,128)} %bitcast.15) | data formatting | bytes 147456

commit v4 on v3

--- a/solution.py
+++ b/solution.py
@@ -301,13 +301,6 @@
         edges_ref[1, pl.ds(d, 1)] = cells_ref[d, pl.ds(leaves - 1, 1)]
     for k in range(2):
         edges_ref[k, pl.ds(6, 2)] = jnp.zeros((2, edges_ref.shape[2]), jnp.float32)
-    pl.semaphore_wait(barrier, greeted + distant * slabs)
-    for around in (0, -1, 1):
-        send(edges_ref.at[1], brims_ref.at[1 - around, 0], around, 1)
-        send(edges_ref.at[0], brims_ref.at[1 - around, 1], around, -1)
-    for around in (-1, 1):
-        send(cells_ref, padded_ref.at[1 - around, :, pl.ds(0, leaves)], around, 0)
-
     for load in loads[3:]:
         load.wait()
 
@@ -350,15 +343,21 @@
     share_ref[...] = jnp.concatenate(
         [portion, jnp.zeros((8, share_ref.shape[1] - rank), jnp.float32)], 1
     )
+    prepare, targets, run = near_steps(padded_ref, stiff_ref, out_ref, work)
+    padded_ref[1, :, pl.ds(0, leaves)] = cells_ref[...]
+    targets()
+    pl.semaphore_wait(barrier, greeted + distant * slabs)
+    for around in (0, -1, 1):
+        send(edges_ref.at[1], brims_ref.at[1 - around, 0], around, 1)
+        send(edges_ref.at[0], brims_ref.at[1 - around, 1], around, -1)
+    for around in (-1, 1):
+        send(cells_ref, padded_ref.at[1 - around, :, pl.ds(0, leaves)], around, 0)
     offsets = far_offsets()
     for q, around in enumerate(offsets):
         send(coefs_ref, windows_ref.at[q, pl.ds(8, leaves)], -around, 0)
         send(coefs_ref.at[pl.ds(leaves - 8, 8)], windows_ref.at[q, pl.ds(0, 8)], -around, 1)
         send(coefs_ref.at[pl.ds(0, 8)], windows_ref.at[q, pl.ds(leaves + 8, 8)], -around, -1)
     lax.fori_loop(0, distant * slabs, share_start, 0)
-
-    prepare, targets, run = near_steps(padded_ref, stiff_ref, out_ref, work)
-    padded_ref[1, :, pl.ds(0, leaves)] = cells_ref[...]
     spare = jnp.zeros((slots - leaves, cells_ref.shape[2]), jnp.float32)
     at = lax.broadcasted_iota(jnp.int32, spare.shape, 0)
 
@@ -371,7 +370,6 @@
                 at == 0, before, jnp.where(at == 1, after, spare)
             )
 
-    targets()
     for copy in copies[:2]:
         copy.wait()
     close(1)
@@ -413,28 +411,46 @@
         [fold(total), jnp.zeros((count * leaves, far_ref.shape[1] - rank), jnp.float32)], 1
     )
 
-    def across(k, carry):
+    def facing(k):
         other = lax.rem(sector + REACH + 1 + k, sectors)
         held = shares_ref[other, 0]
         for p in range(1, slabs):
             held = held + shares_ref[other, p]
-        block = top_ref[other] * listed_ref[0, other].astype(jnp.float32)
-        return carry + fold(split_product(stack_halves(held[:, :rank]), block, True))
-
-    sector_local = lax.fori_loop(0, distant, across, jnp.zeros((8, rank), jnp.float32))
+        return held[:, :rank], top_ref[other] * listed_ref[0, other].astype(jnp.float32)
+
+    def across(k, carry):
+        held, block = facing(k)
+        return carry + fold(split_product(stack_halves(held), block, True))
+
+    sector_local = jnp.zeros((8, rank), jnp.float32)
+    if distant <= 4:
+        if distant > 0:
+            pairs = [facing(k) for k in range(distant)]
+            held, block = (jnp.concatenate(x, 1) for x in zip(*pairs))
+            sector_local = fold(split_product(stack_halves(held), block, True))
+    else:
+        sector_local = lax.fori_loop(0, distant, across, sector_local)
     slab_local = fold(split_product(stack_halves(sector_local), slab_ref[...], True))
     slab_left = stack_halves(slab_local)
 
-    def down(l, carry):
-        local = fold(split_product(slab_left, transfer_ref[l], True))
-        side = [far_ref[pl.ds(leaves * r + l, 1)][:, :rank] for r in range(count)]
-        local = local + jnp.concatenate(side + [jnp.zeros((8 - count, rank), jnp.float32)], 0)
-        spread = fold(split_product(stack_halves(local), basis_ref[l], False))
+    def down(g, carry):
+        first = pl.multiple_of(8 * g, 8)
+        sides = [far_ref[pl.ds(pl.multiple_of(leaves * r + 8 * g, 8), 8)] for r in range(count)]
+        blank = jnp.zeros((8 - count, rank), jnp.float32)
+        drops = [fold(split_product(slab_left, transfer_ref[first + n], True)) for n in range(8)]
+        lefts = [
+            stack_halves(
+                drops[n] + jnp.concatenate([x[n : n + 1, :rank] for x in sides] + [blank], 0)
+            )
+            for n in range(8)
+        ]
+        spreads = [fold(split_product(lefts[n], basis_ref[first + n], False)) for n in range(8)]
         for r in range(count):
-            out_ref[r, pl.ds(l, 1)] = out_ref[r, pl.ds(l, 1)] + spread[r : r + 1]
+            rows = jnp.concatenate([x[r : r + 1] for x in spreads], 0)
+            out_ref[r, pl.ds(first, 8)] = out_ref[r, pl.ds(first, 8)] + rows
         return carry
 
-    lax.fori_loop(0, leaves, down, 0, unroll=8 if leaves % 8 == 0 else 1)
+    lax.fori_loop(0, leaves // 8, down, 0)
 
 
 def exchange(arrays, mask, listed):
@@ -479,7 +495,7 @@
             *[pltpu.VMEM((12, size, size), jnp.bfloat16)] * 4,
         ],
         compiler_params=pltpu.CompilerParams(
-            collective_id=0, has_side_effects=True, vmem_limit_bytes=60 * 1024 * 1024
+            collective_id=0, has_side_effects=True, vmem_limit_bytes=40 * 1024 * 1024
         ),
     )(*arrays, mask, listed)
 

time: 37.8 us -> 34.6 us (0.915)
  Pallas kernels: 36.1 us -> 32.5 us
  local copies, waits for them, and re-layouts: 1.52 us -> 1.94 us
    pallas_call x1, Pallas kernels: 36.1 us -> 32.5 us  [exchange(): pl.pallas_call(exchange_kernel, out_shape=jax.ShapeDtypeStruct((count, le...]
    unnamed x1 -> x5, local copies, waits for them, and re-layouts: 1.52 us -> 1.94 us
where the time goes in v4:
time: 34.6 us; the launch traced here: 34.4 us
  Pallas kernels  32.5 us (94%)
  local copies, waits for them, and re-layouts  1.94 us (6%)
    pallas_call x1, Pallas kernels, exchange(): pl.pallas_call(exchange_kernel, out_shape=jax.ShapeDtypeStruct((count, le...  32.5 us
    unnamed x5, local copies, waits for them, and re-layouts  1.94 us

profile of v4, /device:TPU:0, one launch (start us, length us, event | category | flops | bytes accessed | tf_op | source)
XLA Modules:
  0.0 34.4 jit_solution(884670477913776558)
XLA Ops:
  0.0 0.0 copy-start
  0.0 0.7 %copy-done = s32[1,30]{1,0:T(1,128)S(1)} copy-done((s32[1,30]{1,0:T(1,128)S(1)}, s32[1,30]{1,0:T(1,128)}, u32[]{:S(2)}) %copy-start) | copy-done | bytes 144
  0.7 0.0 copy-start.1
  0.7 0.7 %copy-done.1 = s32[1,16]{1,0:T(1,128)S(1)} copy-done((s32[1,16]{1,0:T(1,128)S(1)}, s32[1,16]{1,0:T(1,128)}, u32[]{:S(2)}) %copy-start.1) | copy-done | bytes 88
  1.3 32.5 %shard_map.100 = f32[3,24,256]{2,1,0:T(8,128)S(1)} custom-call(f32[3,24,256]{2,1,0:T(8,128)} %bitcast.16, f32[3,24,256]{2,1,0:T(8,128)} %bitcast.17, f32[24,256]{1,0:T(8,128)} %bitcast.19, f32[24,64,256]{2,1,0:T(8,128)} %bitcast.12, f32[24,64,64]{2,1,0:T(8,128)} %bitcast.14, f32[64,64]{1,0:T(8,128)} %bitcast.18, f32[30,64,64]{2,1,0:T(8,128)} %bitcast.13, ...), custom_call_target="tpu_custom_call" | custom-call | tf_op jit(solution)/shard_map/pallas_call | solution.py:468
  33.8 0.6 %copy.13 = f32[3,1,24,256]{3,2,1,0:T(8,128)} copy(f32[3,1,24,256]{3,2,1,0:T(8,128)S(1)} %bitcast.11) | data formatting | bytes 147456
Async XLA Ops:
  0.0 0.7 %copy-start = (s32[1,30]{1,0:T(1,128)S(1)}, s32[1,30]{1,0:T(1,128)}, u32[]{:S(2)}) copy-start(s32[1,30]{1,0:T(1,128)} %refs_8_.1) | copy-start | bytes 364
  0.7 0.7 %copy-start.1 = (s32[1,16]{1,0:T(1,128)S(1)}, s32[1,16]{1,0:T(1,128)}, u32[]{:S(2)}) copy-start(s32[1,16]{1,0:T(1,128)} %refs_9_.1) | copy-start | bytes 196

commit v5 on v4

--- a/solution.py
+++ b/solution.py
@@ -158,11 +158,11 @@
 def exchange_kernel(
     *refs,
 ):
-    given, refs = refs[:8], refs[8:]
-    mask_ref, listed_ref, out_ref, *refs = refs
-    here, refs = refs[:8], refs[8:]
+    given, refs = refs[:10], refs[10:]
+    out_ref, *refs = refs
+    here, refs = refs[:10], refs[10:]
     values_ref, offsets_ref, stiff_ref, basis_ref, transfer_ref = here[:5]
-    slab_ref, coupling_ref, top_ref = here[5:]
+    slab_ref, coupling_ref, top_ref, mask_ref, listed_ref = here[5:]
     exchange_steps(
         given,
         here,
@@ -281,7 +281,7 @@
 
     greeted = 0
     for around in (0, -1, 1, *far_offsets()):
-        for along in (-1, 0, 1):
+        for along in (-1, 0, 1) if slabs > 2 else range(slabs):
             if around or along:
                 greet(around, along)
                 greeted += 1
@@ -352,12 +352,6 @@
         send(edges_ref.at[0], brims_ref.at[1 - around, 1], around, -1)
     for around in (-1, 1):
         send(cells_ref, padded_ref.at[1 - around, :, pl.ds(0, leaves)], around, 0)
-    offsets = far_offsets()
-    for q, around in enumerate(offsets):
-        send(coefs_ref, windows_ref.at[q, pl.ds(8, leaves)], -around, 0)
-        send(coefs_ref.at[pl.ds(leaves - 8, 8)], windows_ref.at[q, pl.ds(0, 8)], -around, 1)
-        send(coefs_ref.at[pl.ds(0, 8)], windows_ref.at[q, pl.ds(leaves + 8, 8)], -around, -1)
-    lax.fori_loop(0, distant * slabs, share_start, 0)
     spare = jnp.zeros((slots - leaves, cells_ref.shape[2]), jnp.float32)
     at = lax.broadcasted_iota(jnp.int32, spare.shape, 0)
 
@@ -375,6 +369,12 @@
     close(1)
     prepare(1)
     run((1,), True, 2)
+    offsets = far_offsets()
+    for q, around in enumerate(offsets):
+        send(coefs_ref, windows_ref.at[q, pl.ds(8, leaves)], -around, 0)
+        send(coefs_ref.at[pl.ds(leaves - 8, 8)], windows_ref.at[q, pl.ds(0, 8)], -around, 1)
+        send(coefs_ref.at[pl.ds(0, 8)], windows_ref.at[q, pl.ds(leaves + 8, 8)], -around, -1)
+    lax.fori_loop(0, distant * slabs, share_start, 0)
     for copy in copies[2:8]:
         copy.wait()
     close(0)
@@ -453,7 +453,7 @@
     lax.fori_loop(0, leaves // 8, down, 0)
 
 
-def exchange(arrays, mask, listed):
+def exchange(arrays):
     sectors, slabs = lax.axis_size("blk"), lax.axis_size("along")
     count, leaves, size = arrays[0].shape
     rank = arrays[3].shape[1]
@@ -464,14 +464,14 @@
     links = 8 + 3 * far
     pairs = (sectors - 2 * REACH - 1) * slabs
     hbm = pl.BlockSpec(memory_space=pltpu.HBM)
-    smem = pl.BlockSpec(memory_space=pltpu.SMEM)
     return pl.pallas_call(
         exchange_kernel,
         out_shape=jax.ShapeDtypeStruct((count, leaves, size), jnp.float32),
-        in_specs=[hbm] * len(arrays) + [smem] * 2,
+        in_specs=[hbm] * len(arrays),
         out_specs=pl.BlockSpec(memory_space=pltpu.VMEM),
         scratch_shapes=[
-            *[pltpu.VMEM(x.shape, x.dtype) for x in arrays],
+            *[pltpu.VMEM(x.shape, x.dtype) for x in arrays[:8]],
+            *[pltpu.SMEM(x.shape, x.dtype) for x in arrays[8:]],
             pltpu.VMEM((6, leaves, size), jnp.float32),
             pltpu.VMEM((2, 8, size), jnp.float32),
             pltpu.VMEM((3, 6, slots, size), jnp.float32),
@@ -497,7 +497,7 @@
         compiler_params=pltpu.CompilerParams(
             collective_id=0, has_side_effects=True, vmem_limit_bytes=40 * 1024 * 1024
         ),
-    )(*arrays, mask, listed)
+    )(*arrays)
 
 
 def body(
@@ -521,9 +521,11 @@
         slab_transfer_matrices[0, 0],
         leaf_coupling_matrices[0],
         top_coupling[0],
+        leaf_admissible_mask,
+        top_admissible,
     )
     arrays = tuple(pltpu.with_memory_space_constraint(x, pltpu.HBM) for x in arrays)
-    return exchange(arrays, leaf_admissible_mask, top_admissible)[:, None]
+    return exchange(arrays)[:, None]
 
 
 def solution(mesh):

time: 34.6 us -> 32.3 us (0.934)
  local copies, waits for them, and re-layouts: 1.94 us -> 0.64 us
  Pallas kernels: 32.5 us -> 31.5 us
    unnamed x5 -> x1, local copies, waits for them, and re-layouts: 1.94 us -> 0.64 us
    pallas_call x1, Pallas kernels: 32.5 us -> 31.5 us  [exchange(): pl.pallas_call(exchange_kernel, out_shape=jax.ShapeDtypeStruct((count, le...]
where the time goes in v5:
time: 32.3 us; the launch traced here: 32.1 us
  Pallas kernels  31.5 us (98%)
  local copies, waits for them, and re-layouts  0.64 us (2%)
    pallas_call x1, Pallas kernels, exchange(): pl.pallas_call(exchange_kernel, out_shape=jax.ShapeDtypeStruct((count, le...  31.5 us

profile of v5, /device:TPU:0, one launch (start us, length us, event | category | flops | bytes accessed | tf_op | source)
XLA Modules:
  0.0 32.1 jit_solution(5585008783650928610)
XLA Ops:
  0.0 31.5 %shard_map.100 = f32[3,24,256]{2,1,0:T(8,128)S(1)} custom-call(f32[3,24,256]{2,1,0:T(8,128)} %bitcast.16, f32[3,24,256]{2,1,0:T(8,128)} %bitcast.17, f32[24,256]{1,0:T(8,128)} %bitcast.19, f32[24,64,256]{2,1,0:T(8,128)} %bitcast.12, f32[24,64,64]{2,1,0:T(8,128)} %bitcast.14, f32[64,64]{1,0:T(8,128)} %bitcast.18, f32[30,64,64]{2,1,0:T(8,128)} %bitcast.13, ...), custom_call_target="tpu_custom_call" | custom-call | tf_op jit(solution)/shard_map/pallas_call | solution.py:467
  31.5 0.6 %copy.13 = f32[3,1,24,256]{3,2,1,0:T(8,128)} copy(f32[3,1,24,256]{3,2,1,0:T(8,128)S(1)} %bitcast.11) | data formatting | bytes 147456

commit v6 on v5

--- a/solution.py
+++ b/solution.py
@@ -368,7 +368,7 @@
         copy.wait()
     close(1)
     prepare(1)
-    run((1,), True, 2)
+    run((1,), True, 4)
     offsets = far_offsets()
     for q, around in enumerate(offsets):
         send(coefs_ref, windows_ref.at[q, pl.ds(8, leaves)], -around, 0)

time: 32.3 us -> 32.1 us (level)
  no operation moved by 1% of the time
where the time goes in v6:
time: 32.1 us; the launch traced here: 32 us
  Pallas kernels  31.3 us (98%)
  local copies, waits for them, and re-layouts  0.64 us (2%)
    pallas_call x1, Pallas kernels, exchange(): pl.pallas_call(exchange_kernel, out_shape=jax.ShapeDtypeStruct((count, le...  31.3 us

profile of v6, /device:TPU:0, one launch (start us, length us, event | category | flops | bytes accessed | tf_op | source)
XLA Modules:
  0.0 32.0 jit_solution(11959082146262307543)
XLA Ops:
  0.0 31.3 %shard_map.100 = f32[3,24,256]{2,1,0:T(8,128)S(1)} custom-call(f32[3,24,256]{2,1,0:T(8,128)} %bitcast.16, f32[3,24,256]{2,1,0:T(8,128)} %bitcast.17, f32[24,256]{1,0:T(8,128)} %bitcast.19, f32[24,64,256]{2,1,0:T(8,128)} %bitcast.12, f32[24,64,64]{2,1,0:T(8,128)} %bitcast.14, f32[64,64]{1,0:T(8,128)} %bitcast.18, f32[30,64,64]{2,1,0:T(8,128)} %bitcast.13, ...), custom_call_target="tpu_custom_call" | custom-call | tf_op jit(solution)/shard_map/pallas_call | solution.py:467
  31.3 0.6 %copy.13 = f32[3,1,24,256]{3,2,1,0:T(8,128)} copy(f32[3,1,24,256]{3,2,1,0:T(8,128)S(1)} %bitcast.11) | data formatting | bytes 147456
